TPU v7x, 8 devices: a whole 2x2x1 slice. The times are simulated.
8 devices in a mesh: dp: 1 (over z), tp: 8 (over y, x, core).
Axes of the slice: x: 2, y: 2, z: 1, core: 2. Of those that a mesh axis runs over, the one named last changes fastest.
Arguments:
- tokens: bfloat16 [32, 64, 5120], P('dp')
- seq_lens: int32 [32], P('dp')
- w_q: bfloat16 [5120, 5120], P(None, 'tp')
- w_k: bfloat16 [5120, 1024], P(None, 'tp')
- w_v: bfloat16 [5120, 1024], P(None, 'tp')
- w_o: bfloat16 [5120, 5120], P('tp')
- g_q: bfloat16 [5120], P('tp')
- g_k: bfloat16 [1024], P('tp')
- g_attn: bfloat16 [5120], replicated
- g_mlp: bfloat16 [5120], replicated
- w_gate: bfloat16 [5120, 27648], P(None, 'tp')
- w_up: bfloat16 [5120, 27648], P(None, 'tp')
- w_down: bfloat16 [27648, 5120], P('tp')
Outputs:
- output 1: bfloat16 [32, 64, 5120], P('dp')
- output 2: bfloat16 [32, 8, 64, 128], P('dp', 'tp')
- output 3: bfloat16 [32, 8, 64, 128], P('dp', 'tp')
All inputs are finite; a program needn't handle non-finite values.
Results may differ from a plain program's by a relative error of at most 0.0157053.
Values are sent between devices in bfloat16 or wider.
A program may use at most 1 GiB of HBM per device.

v0:
```python
import jax
import jax.numpy as jnp
from jax import lax
from jax.sharding import PartitionSpec as P

HEAD_DIM = 128
ROPE_BASE = 500000.0
NORM_EPS = 1e-6


def rope_tables(seq_len, head_dim):
    half_dim = head_dim // 2
    inv_freq = ROPE_BASE ** (-2.0 * jnp.arange(half_dim, dtype=jnp.float32) / head_dim)
    angles = jnp.arange(seq_len, dtype=jnp.float32)[:, None] * inv_freq[None, :]
    angles = jnp.concatenate([angles, angles], axis=-1)
    return jnp.cos(angles), jnp.sin(angles)


def apply_rope(vecs, cos_tab, sin_tab, head_axes):
    half_dim = vecs.shape[-1] // 2
    table_shape = (cos_tab.shape[0],) + (1,) * head_axes + (cos_tab.shape[1],)
    rotated = jnp.concatenate([-vecs[..., half_dim:], vecs[..., :half_dim]], axis=-1)
    return vecs * cos_tab.reshape(table_shape) + rotated * sin_tab.reshape(table_shape)


def rms_scale(vals):
    return lax.rsqrt(jnp.mean(vals * vals, axis=-1, keepdims=True) + NORM_EPS)


def post_norm(base, branch, gain):
    branch32 = branch.astype(jnp.float32)
    return (base.astype(jnp.float32) + branch32 * rms_scale(branch32) * gain.astype(jnp.float32)).astype(jnp.bfloat16)


def solution(mesh):
    tp_size = mesh.shape['tp']

    def local_layer(tokens, seq_lens, w_q, w_k, w_v, w_o, g_q, g_k, g_attn, g_mlp, w_gate, w_up, w_down):
        prompts, seq_len = tokens.shape[0], tokens.shape[1]
        kv_local = w_k.shape[1] // HEAD_DIM
        group_size = w_q.shape[1] // w_k.shape[1]
        q_raw = jnp.einsum('bsd,dn->bsn', tokens, w_q, preferred_element_type=jnp.float32)
        k_raw = jnp.einsum('bsd,dn->bsn', tokens, w_k, preferred_element_type=jnp.float32)
        v_new = jnp.einsum('bsd,dn->bsn', tokens, w_v, preferred_element_type=jnp.float32).astype(jnp.bfloat16)
        q_sumsq = lax.psum(jnp.sum(q_raw * q_raw, axis=-1, keepdims=True), 'tp')
        k_sumsq = lax.psum(jnp.sum(k_raw * k_raw, axis=-1, keepdims=True), 'tp')
        q_norm = q_raw * lax.rsqrt(q_sumsq / (w_q.shape[1] * tp_size) + NORM_EPS) * g_q.astype(jnp.float32)
        k_norm = k_raw * lax.rsqrt(k_sumsq / (w_k.shape[1] * tp_size) + NORM_EPS) * g_k.astype(jnp.float32)
        cos_tab, sin_tab = rope_tables(seq_len, HEAD_DIM)
        queries = apply_rope(q_norm.reshape(prompts, seq_len, kv_local, group_size, HEAD_DIM), cos_tab, sin_tab, 2).astype(jnp.bfloat16)
        keys_new = apply_rope(k_norm.reshape(prompts, seq_len, kv_local, HEAD_DIM), cos_tab, sin_tab, 1).astype(jnp.bfloat16)
        k_cache = jnp.transpose(keys_new, (0, 2, 1, 3))
        v_cache = jnp.transpose(v_new.reshape(prompts, seq_len, kv_local, HEAD_DIM), (0, 2, 1, 3))
        scores = jnp.einsum('bsgrd,bgtd->bgrst', queries, k_cache, preferred_element_type=jnp.float32) * HEAD_DIM ** -0.5
        positions = jnp.arange(seq_len)
        allowed = (positions[None, None, :] <= positions[None, :, None]) & (positions[None, None, :] < seq_lens[:, None, None])
        scores = jnp.where(allowed[:, None, None], scores, -1e30)
        attn_probs = jax.nn.softmax(scores, axis=-1).astype(jnp.bfloat16)
        attn_out = jnp.einsum('bgrst,bgtd->bsgrd', attn_probs, v_cache, preferred_element_type=jnp.float32).astype(jnp.bfloat16)
        attn_part = jnp.einsum('bsn,nd->bsd', attn_out.reshape(prompts, seq_len, -1), w_o, preferred_element_type=jnp.float32).astype(jnp.bfloat16)
        attn_proj = lax.psum(attn_part, 'tp')
        hidden = post_norm(tokens, attn_proj, g_attn)
        gate_pre = jnp.einsum('bsd,df->bsf', hidden, w_gate, preferred_element_type=jnp.float32)
        up_proj = jnp.einsum('bsd,df->bsf', hidden, w_up, preferred_element_type=jnp.float32)
        act_out = (jax.nn.silu(gate_pre) * up_proj).astype(jnp.bfloat16)
        mlp_part = jnp.einsum('bsf,fd->bsd', act_out, w_down, preferred_element_type=jnp.float32).astype(jnp.bfloat16)
        mlp_out = lax.psum(mlp_part, 'tp')
        out_hidden = post_norm(hidden, mlp_out, g_mlp)
        return out_hidden, k_cache, v_cache

    return jax.shard_map(local_layer, mesh=mesh, in_specs=(P('dp', None, None), P('dp'), P(None, 'tp'), P(None, 'tp'), P(None, 'tp'), P('tp', None), P('tp'), P('tp'), P(), P(), P(None, 'tp'), P(None, 'tp'), P('tp', None)), out_specs=(P('dp', None, None), P('dp', 'tp', None, None), P('dp', 'tp', None, None)), check_vma=False)
```

profile of v0, /device:TPU:0, one launch (start us, length us, event | category | flops | bytes accessed | tf_op | source)
XLA Modules:
  0.0 997.4 jit_solution(1708911319414322136)
XLA Ops:
  7.3 22.7 %multiply_reduce_fusion = (f32[32,64]{1,0:T(8,128)S(1)}, f32[32,64,640]{2,1,0:T(8,128)}) fusion(bf16[32,64,5120]{2,1,0:T(8,128)(2,1)} %param.13, bf16[5120,640]{1,0:T(8,128)(2,1)} %param.15), kind=kOutput, calls=%fused_computation.34 | convolution fusion | flops 13424392192 | bytes 32776192 | tf_op jit(solution)/shard_map/bsd,dn->bsn/dot_general | solution.py:42
  30.0 5.9 multiply_reduce_fusion.1
  36.0 25.5 %all-reduce = (f32[32,64,1]{1,0,2:T(8,128)S(1)}, f32[32,64,1]{1,0,2:T(8,128)S(1)}) all-reduce(f32[32,64,1]{1,0,2:T(8,128)S(1)} %bitcast.101, f32[32,64,1]{1,0,2:T(8,128)S(1)} %bitcast.102), channel_id=1, replica_groups=mesh['dp'=1,'tp'=8] {'tp'}, use_global_device_ids=true, to_apply=%region_3.0 | all-reduce | flops 4096 | bytes 32768 | tf_op jit(solution)/shard_map/psum | solution.py:45
  61.5 5.4 multiply_multiply_fusion
  66.9 7.3 reshape.216
  74.2 7.4 reshape.215
  82.5 10.8 %fusion.19 = (f32[32,64,5,64]{3,2,1,0:T(8,128)S(1)}, f32[32,64,5,64]{3,2,1,0:T(8,128)}) fusion(f32[32,64,1,5,128]{4,3,1,0,2:T(8,128)} %reshape.216), kind=kLoop, calls=%fused_computation.23 | loop fusion | flops 655360 | bytes 10485760 | tf_op jit(solution)/shard_map/concatenate | solution.py:22
  93.4 11.1 %fusion.41 = bf16[32,64,128]{2,1,0:T(8,128)(2,1)} fusion(bf16[32,64,5120]{2,1,0:T(8,128)(2,1)} %param.13, bf16[5120,128]{1,0:T(8,128)(2,1)} %param.17), kind=kOutput, calls=%fused_computation.50 | convolution fusion | flops 2684616704 | bytes 22806528 | tf_op jit(solution)/shard_map/bsd,dn->bsn/dot_general | solution.py:44
  105.5 5.5 fusion.21
  111.0 2.3 fusion.26
  117.1 4.4 copy.24
  121.5 7.1 reshape.218
  128.6 24.4 %convolution_convert_fusion = bf16[32,64,5120]{2,1,0:T(8,128)(2,1)} fusion(bf16[32,64,640]{2,1,0:T(8,128)(2,1)} %reshape.218, bf16[640,5120]{1,0:T(8,128)(2,1)} %param.18), kind=kOutput, calls=%fused_computation.20 | convolution fusion | flops 13432258560 | bytes 30146560 | tf_op jit(solution)/shard_map/bsn,nd->bsd/dot_general | solution.py:60
  153.8 251.6 %all-reduce.4.cloned.1.call-done = bf16[32,64,5120]{2,1,0:T(8,128)(2,1)} async-done(((bf16[32,64,5120]{2,1,0:T(8,128)(2,1)}), bf16[32,64,5120]{2,1,0:T(8,128)(2,1)}) %all-reduce.4.cloned.1.call-update) | async-done | bytes 20971536 | tf_op jit(solution)/shard_map/psum | solution.py:61
  405.4 9.4 fusion
  414.8 3.7 copy-done.2
  418.5 20.3 %fusion.3 = bf16[32,64,5120]{2,1,0:T(8,128)(2,1)} fusion(bf16[32,64,5120]{2,1,0:T(8,128)(2,1)S(1)} %copy-done.2, bf16[32,64,5120]{2,1,0:T(8,128)(2,1)} %param.13, f32[5120]{0:T(1024)S(1)} %convert_element_type.76, f32[32,64]{1,0:T(8,128)S(1)} %add_rsqrt_fusion.1), kind=kLoop, calls=%fused_computation.7 | loop fusion | flops 62914560 | bytes 62943232 | tf_op jit(solution)/shard_map/convert_element_type | solution.py:32
  438.8 87.9 %fusion.10 = f32[32,64,3456]{2,1,0:T(8,128)} fusion(bf16[32,64,5120]{2,1,0:T(8,128)(2,1)} %fusion.3, bf16[5120,3456]{1,0:T(8,128)(2,1)} %param.24), kind=kOutput, calls=%fused_computation.14 | convolution fusion | flops 72477573120 | bytes 84672512 | tf_op jit(solution)/shard_map/bsd,df->bsf/dot_general | solution.py:64
  526.6 94.0 %multiply_convert_fusion = bf16[32,64,3456]{2,1,0:T(8,128)(2,1)} fusion(f32[32,64,3456]{2,1,0:T(8,128)} %fusion.10, bf16[32,64,5120]{2,1,0:T(8,128)(2,1)} %fusion.3, bf16[5120,3456]{1,0:T(8,128)(2,1)} %param.23), kind=kOutput, calls=%fused_computation.18 | convolution fusion | flops 72520040448 | bytes 98828288 | tf_op jit(solution)/shard_map/bsd,df->bsf/dot_general | solution.py:63
  620.7 84.5 %fusion.16 = bf16[32,64,5120]{2,1,0:T(8,128)(2,1)} fusion(bf16[32,64,3456]{2,1,0:T(8,128)(2,1)} %multiply_convert_fusion, bf16[3456,5120]{1,0:T(8,128)(2,1)} %param.25), kind=kOutput, calls=%fused_computation.19 | convolution fusion | flops 72488058880 | bytes 70516736 | tf_op jit(solution)/shard_map/bsf,fd->bsd/dot_general | solution.py:66
  705.9 250.8 %all-reduce.6.cloned.1.call-done = bf16[32,64,5120]{2,1,0:T(8,128)(2,1)} async-done(((bf16[32,64,5120]{2,1,0:T(8,128)(2,1)}), bf16[32,64,5120]{2,1,0:T(8,128)(2,1)}) %all-reduce.6.cloned.1.call-update) | async-done | bytes 20971536 | tf_op jit(solution)/shard_map/psum | solution.py:67
  956.6 9.2 fusion.4
  965.9 3.9 copy-done.3
  969.8 20.4 %fusion.7 = bf16[32,64,5120]{2,1,0:T(8,128)(2,1)} fusion(bf16[32,64,5120]{2,1,0:T(8,128)(2,1)S(1)} %copy-done.3, bf16[32,64,5120]{2,1,0:T(8,128)(2,1)} %fusion.3, f32[5120]{0:T(1024)S(1)} %convert_element_type.82, f32[32,64]{1,0:T(8,128)S(1)} %add_rsqrt_fusion), kind=kLoop, calls=%fused_computation.11 | loop fusion | flops 62914560 | bytes 62943232 | tf_op jit(solution)/shard_map/convert_element_type | solution.py:32
  (49 shorter events, 7.2 us)
Async XLA Ops:
  7.2 22.8 %copy-start = (bf16[5120,128]{1,0:T(8,128)(2,1)S(1)}, bf16[5120,128]{1,0:T(8,128)(2,1)}, u32[]{:S(2)}) copy-start(bf16[5120,128]{1,0:T(8,128)(2,1)} %param.16) | copy-start | bytes 3932164
  7.2 398.2 %all-reduce.4.cloned.1.call-start = ((), (), s32[]{:S(2)}) async-start(), calls=%async_computation | async-start | bytes 41943040 | tf_op jit(solution)/shard_map/psum | solution.py:61
  7.2 22.8 %copy-start.4 = (bf16[32,64,5120]{2,1,0:T(8,128)(2,1)S(1)}, bf16[32,64,5120]{2,1,0:T(8,128)(2,1)}, u32[]{:S(2)}) copy-start(bf16[32,64,5120]{2,1,0:T(8,128)(2,1)} %param.13) | copy-start | bytes 62914564
  30.0 6.0 copy-start.8
  74.2 7.4 copy-start.10
  82.5 10.8 %copy-start.9 = (s32[32]{0:T(128)S(1)}, s32[32]{0:T(128)}, u32[]{:S(2)}) copy-start(s32[32]{0:T(128)} %param.14) | copy-start | bytes 388
  93.3 12.2 %slice-start = ((s8[8388608]{0:T(1024)(128)(4,1)}), s8[4194304]{0:T(1024)(128)(4,1)S(1)}, s32[]{:S(2)}) async-start(s8[8388608]{0:T(1024)(128)(4,1)} %bitcast.98), calls=%async_computation.2 | async-start | bytes 8388608
  93.4 12.1 %slice-start.1 = ((s8[8388608]{0:T(1024)(128)(4,1)}), s8[4194304]{0:T(1024)(128)(4,1)S(1)}, s32[]{:S(2)}) async-start(s8[8388608]{0:T(1024)(128)(4,1)} %bitcast.98), calls=%async_computation.3 | async-start | bytes 8388608
  105.5 5.5 copy-start.5
  111.0 4.3 copy-start.11
  153.1 0.7 copy-start.6
  153.1 803.5 %all-reduce.6.cloned.1.call-start = ((), (), s32[]{:S(2)}) async-start(), calls=%async_computation.1 | async-start | bytes 41943040 | tf_op jit(solution)/shard_map/psum | solution.py:67
  405.3 13.1 %copy-start.2 = (bf16[32,64,5120]{2,1,0:T(8,128)(2,1)S(1)}, bf16[32,64,5120]{2,1,0:T(8,128)(2,1)}, u32[]{:S(2)}) copy-start(bf16[32,64,5120]{2,1,0:T(8,128)(2,1)} %all-reduce.4.cloned.1.call-done) | copy-start | bytes 62914564
  705.2 0.7 copy-start.7
  956.6 13.1 %copy-start.3 = (bf16[32,64,5120]{2,1,0:T(8,128)(2,1)S(1)}, bf16[32,64,5120]{2,1,0:T(8,128)(2,1)}, u32[]{:S(2)}) copy-start(bf16[32,64,5120]{2,1,0:T(8,128)(2,1)} %all-reduce.6.cloned.1.call-done) | copy-start | bytes 62914564
  969.8 20.4 %copy-start.1 = (bf16[5120,128]{1,0:T(8,128)(2,1)S(1)}, bf16[5120,128]{1,0:T(8,128)(2,1)}, u32[]{:S(2)}) copy-start(bf16[5120,128]{1,0:T(8,128)(2,1)} %param.16) | copy-start | bytes 3932164
Sparse Core Ops, SparseCore 0:
  153.2 252.0 all-reduce.3
  705.3 251.2 all-reduce.5
where the time goes:
time: 1000 us; the launch traced here: 997 us
  waiting for transfers between devices  502 us (50%)
  matrix products  335 us (34%)
  other arithmetic  85 us (8%)
  local copies, waits for them, and re-layouts  35.1 us (4%)
  blocking collectives  25.5 us (3%)
  between operations  14.7 us (1%)
    psum x1, waiting for transfers between devices, local_layer(): attn_proj = lax.psum(attn_part, 'tp')  252 us
    psum x1, waiting for transfers between devices, local_layer(): mlp_out = lax.psum(mlp_part, 'tp')  251 us
    dot_general x1, matrix products, local_layer(): jnp.einsum('bsd,df->bsf', hidden, w_gate, preferred_element_type=jnp.floa...  94 us
    dot_general x1, matrix products, local_layer(): jnp.einsum('bsd,df->bsf', hidden, w_up, preferred_element_type=jnp.float32)  87.9 us
    dot_general x1, matrix products, local_layer(): jnp.einsum('bsf,fd->bsd', act_out, w_down, preferred_element_type=jnp.flo...  84.5 us
    convert_element_type x2, other arithmetic, post_norm(): (base.astype(jnp.float32) + branch32 * rms_scale(branch32) * gain.astype(...  40.7 us
    psum x1, blocking collectives, local_layer(): q_sumsq = lax.psum(jnp.sum(q_raw * q_raw, axis=-1, keepdims=True), 'tp')  25.5 us
    dot_general x1, matrix products, local_layer(): jnp.einsum('bsn,nd->bsd', attn_out.reshape(prompts, seq_len, -1), w_o, pr...  24.4 us
  transfers between devices with their start and end apart: 2, of which 2 were waited for; matrix products, arithmetic and copies ran while one was open for 0% of the time, Pallas kernels for 0%

commit v1 on v0

v1 whole, which is shorter than its diff:
```python
import jax
import jax.numpy as jnp
from jax import lax
from jax.experimental import pallas as pl
from jax.experimental.pallas import tpu as pltpu
from jax.sharding import PartitionSpec as P

HEAD_DIM = 128
ROPE_BASE = 500000.0
NORM_EPS = 1e-6
CHUNKS = 4


def rope_tables(seq_len, head_dim):
    half_dim = head_dim // 2
    inv_freq = ROPE_BASE ** (-2.0 * jnp.arange(half_dim, dtype=jnp.float32) / head_dim)
    angles = jnp.arange(seq_len, dtype=jnp.float32)[:, None] * inv_freq[None, :]
    cos, sin = jnp.cos(angles), jnp.sin(angles)
    return jnp.concatenate([cos, cos], axis=-1), jnp.concatenate([-sin, sin], axis=-1)


def rms_scale(vals):
    return lax.rsqrt(jnp.mean(vals * vals, axis=-1, keepdims=True) + NORM_EPS)


def post_norm(base, branch, gain):
    branch32 = branch.astype(jnp.float32)
    return (base.astype(jnp.float32) + branch32 * rms_scale(branch32) * gain.astype(jnp.float32)).astype(jnp.bfloat16)


def attn_kernel(seq_len, group, per_step, lens_ref, q_ref, k_ref, v_ref, iq_ref, ik_ref, gq_ref, gk_ref, cos_ref, sin_ref, o_ref, kc_ref):
    step = pl.program_id(0)
    cos, sin = cos_ref[...], sin_ref[...]
    gk = gk_ref[...].astype(jnp.float32)

    def rope(t):
        return t * cos + pltpu.roll(t, HEAD_DIM // 2, 1) * sin

    row = lax.broadcasted_iota(jnp.int32, (seq_len, seq_len), 0)
    col = lax.broadcasted_iota(jnp.int32, (seq_len, seq_len), 1)
    for b in range(per_step):
        rows = pl.ds(b * seq_len, seq_len)
        keys = rope(k_ref[rows, :] * ik_ref[rows, :] * gk).astype(jnp.bfloat16)
        kc_ref[rows, :] = keys
        vals = v_ref[rows, :]
        inv_q = iq_ref[rows, :]
        qs = []
        for h in range(group):
            cols = pl.ds(h * HEAD_DIM, HEAD_DIM)
            qs.append(rope(q_ref[rows, cols] * inv_q * gq_ref[:, cols].astype(jnp.float32)).astype(jnp.bfloat16))
        queries = jnp.concatenate(qs, axis=0)
        scores = lax.dot_general(queries, keys, (((1,), (1,)), ((), ())), preferred_element_type=jnp.float32) * HEAD_DIM ** -0.5
        allowed = (col <= row) & (col < lens_ref[step * per_step + b])
        allowed = jnp.concatenate([allowed.astype(jnp.int32)] * group, axis=0) > 0
        scores = jnp.where(allowed, scores, -1e30)
        top = jnp.max(scores, axis=-1, keepdims=True)
        e = jnp.exp(scores - top)
        probs = (e / jnp.sum(e, axis=-1, keepdims=True)).astype(jnp.bfloat16)
        out = jnp.dot(probs, vals, preferred_element_type=jnp.float32).astype(jnp.bfloat16)
        for h in range(group):
            o_ref[rows, pl.ds(h * HEAD_DIM, HEAD_DIM)] = out[h * seq_len:(h + 1) * seq_len, :]


def attention(seq_lens, q_raw, k_raw, v, inv_q, inv_k, g_q, g_k, cos, sin, seq_len):
    tokens, width = q_raw.shape
    prompts = tokens // seq_len
    per_step = 4 if prompts % 4 == 0 else 1
    rows = per_step * seq_len
    group = width // HEAD_DIM
    def rs(w):
        return pl.BlockSpec((rows, w), lambda i, lens: (i, 0))
    def full(shape):
        return pl.BlockSpec(shape, lambda i, lens: (0, 0))
    import functools
    return pl.pallas_call(
        functools.partial(attn_kernel, seq_len, group, per_step),
        grid_spec=pltpu.PrefetchScalarGridSpec(
            num_scalar_prefetch=1,
            grid=(prompts // per_step,),
            in_specs=[rs(width), rs(HEAD_DIM), rs(HEAD_DIM), rs(1), rs(1), full((1, width)), full((1, HEAD_DIM)), full((seq_len, HEAD_DIM)), full((seq_len, HEAD_DIM))],
            out_specs=[rs(width), rs(HEAD_DIM)],
        ),
        out_shape=[jax.ShapeDtypeStruct((tokens, width), jnp.bfloat16), jax.ShapeDtypeStruct((tokens, HEAD_DIM), jnp.bfloat16)],
        cost_estimate=pl.CostEstimate(flops=4 * tokens * seq_len * width, bytes_accessed=tokens * width * 6, transcendentals=tokens * seq_len * group),
    )(seq_lens, q_raw, k_raw, v, inv_q, inv_k, g_q[None], g_k[None], cos, sin)


def solution(mesh):
    tp_size = mesh.shape['tp']

    def local_layer(tokens, seq_lens, w_q, w_k, w_v, w_o, g_q, g_k, g_attn, g_mlp, w_gate, w_up, w_down):
        prompts, seq_len, width = tokens.shape
        x = tokens.reshape(prompts * seq_len, width)
        me = lax.axis_index('tp')
        f32 = dict(preferred_element_type=jnp.float32)
        q_raw = jnp.dot(x, w_q, **f32)
        k_raw = jnp.dot(x, w_k, **f32)
        v = jnp.dot(x, w_v, **f32).astype(jnp.bfloat16)
        q_sumsq, k_sumsq = lax.psum((jnp.sum(q_raw * q_raw, axis=-1), jnp.sum(k_raw * k_raw, axis=-1)), 'tp')
        inv_q = lax.rsqrt(q_sumsq / (w_q.shape[1] * tp_size) + NORM_EPS)[:, None]
        inv_k = lax.rsqrt(k_sumsq / (w_k.shape[1] * tp_size) + NORM_EPS)[:, None]
        cos, sin = rope_tables(seq_len, HEAD_DIM)
        o, keys = attention(seq_lens, q_raw, k_raw, v, inv_q, inv_k, g_q, g_k, cos, sin, seq_len)
        k_cache = keys.reshape(prompts, 1, seq_len, HEAD_DIM)
        v_cache = v.reshape(prompts, 1, seq_len, HEAD_DIM)

        size = prompts * seq_len // CHUNKS
        own = size // tp_size
        outs = []
        hs = []
        for c in range(CHUNKS):
            part = jnp.dot(lax.slice_in_dim(o, c * size, (c + 1) * size), w_o, **f32).astype(jnp.bfloat16)
            a_own = lax.psum_scatter(part, 'tp', scatter_dimension=0, tiled=True)
            if hs:
                a_own, _ = lax.optimization_barrier((a_own, hs[-1][0]))
            x_own = lax.dynamic_slice_in_dim(x, c * size + me * own, own)
            h_own = post_norm(x_own, a_own, g_attn)
            hs.append((h_own, lax.all_gather(h_own, 'tp', axis=0, tiled=True)))
        for c in range(CHUNKS):
            h_own, h = hs[c]
            gate = jnp.dot(h, w_gate, **f32)
            up = jnp.dot(h, w_up, **f32)
            act = (jax.nn.silu(gate) * up).astype(jnp.bfloat16)
            part = jnp.dot(act, w_down, **f32).astype(jnp.bfloat16)
            m_own = lax.psum_scatter(part, 'tp', scatter_dimension=0, tiled=True)
            if outs:
                m_own, _ = lax.optimization_barrier((m_own, y_own))
            y_own = post_norm(h_own, m_own, g_mlp)
            outs.append(lax.all_gather(y_own, 'tp', axis=0, tiled=True))
        y = jnp.concatenate(outs, axis=0).reshape(prompts, seq_len, width)
        return y, k_cache, v_cache

    return jax.shard_map(local_layer, mesh=mesh, in_specs=(P('dp', None, None), P('dp'), P(None, 'tp'), P(None, 'tp'), P(None, 'tp'), P('tp', None), P('tp'), P('tp'), P(), P(), P(None, 'tp'), P(None, 'tp'), P('tp', None)), out_specs=(P('dp', None, None), P('dp', 'tp', None, None), P('dp', 'tp', None, None)), check_vma=False)
```

time: 1000 us -> 886 us (0.89)
  waiting for transfers between devices: 502 us -> 374 us
  matrix products: 335 us -> 390 us
  other arithmetic: 85 us -> 47.2 us
  local copies, waits for them, and re-layouts: 35.1 us -> 12.7 us
  Pallas kernels: 0 us -> 13.2 us
    psum x2 -> x0, waiting for transfers between devices: 502 us -> none  [the longest x1 252 us: local_layer(): attn_proj = lax.psum(attn_part, 'tp')]
    reduce_scatter x0 -> x8, waiting for transfers between devices: none -> 196 us  [the longest x4 160 us: local_layer(): a_own = lax.psum_scatter(part, 'tp', scatter_dimension=0, tiled=True)]
    all_gather x0 -> x8, waiting for transfers between devices: none -> 178 us  [the longest x4 144 us: local_layer(): outs.append(lax.all_gather(y_own, 'tp', axis=0, tiled=True))]
    dot_general x9 -> x19, matrix products: 335 us -> 390 us  [the longest x4 107 us: local_layer(): gate = jnp.dot(h, w_gate, **f32)]
    convert_element_type x2 -> x8, other arithmetic: 40.7 us -> 18.7 us  [post_norm(): (base.astype(jnp.float32) + branch32 * rms_scale(branch32) * gain.astype(...]
    reshape x3 -> x0, local copies, waits for them, and re-layouts: 21.8 us -> none  [the longest x2 14.7 us: local_layer(): q_norm.reshape(prompts, seq_len, kv_local, group_size, HEAD_DIM)]
    pallas_call x0 -> x1, Pallas kernels: none -> 13.2 us  [attention(): pl.pallas_call(functools.partial(attn_kernel, seq_len, group, per_step),...]
  transfers between devices with their start and end apart: 2 -> 16, of which waited for: 2 -> 10; matrix products, arithmetic and copies ran while one was open for 0% -> 42% of each run, Pallas kernels for 0% -> 0%
where the time goes in v1:
time: 886 us; the launch traced here: 879 us
  matrix products  390 us (44%)
  waiting for transfers between devices  374 us (42%)
  other arithmetic  47.2 us (5%)
  blocking collectives  25.4 us (3%)
  between operations  14.7 us (2%)
  Pallas kernels  13.2 us (1%)
  local copies, waits for them, and re-layouts  12.7 us (1%)
    reduce_scatter x4, waiting for transfers between devices, local_layer(): a_own = lax.psum_scatter(part, 'tp', scatter_dimension=0, tiled=True)  160 us
    all_gather x4, waiting for transfers between devices, local_layer(): outs.append(lax.all_gather(y_own, 'tp', axis=0, tiled=True))  144 us
    dot_general x4, matrix products, local_layer(): gate = jnp.dot(h, w_gate, **f32)  107 us
    dot_general x4, matrix products, local_layer(): up = jnp.dot(h, w_up, **f32)  105 us
    dot_general x4, matrix products, local_layer(): part = jnp.dot(act, w_down, **f32).astype(jnp.bfloat16)  97.9 us
    dot_general x4, matrix products, local_layer(): jnp.dot(lax.slice_in_dim(o, c * size, (c + 1) * size), w_o, **f32)  38.7 us
    reduce_scatter x4, waiting for transfers between devices, local_layer(): m_own = lax.psum_scatter(part, 'tp', scatter_dimension=0, tiled=True)  36.1 us
    all_gather x4, waiting for transfers between devices, local_layer(): hs.append((h_own, lax.all_gather(h_own, 'tp', axis=0, tiled=True)))  33 us
  transfers between devices with their start and end apart: 16, of which 10 were waited for; matrix products, arithmetic and copies ran while one was open for 42% of the time, Pallas kernels for 0%

profile of v1, /device:TPU:0, one launch (start us, length us, event | category | flops | bytes accessed | tf_op | source)
XLA Modules:
  0.0 879.0 jit_solution(1752715446426760380)
XLA Ops:
  32.2 19.9 %multiply_reduce_fusion = (f32[2048]{0:T(1024)S(1)}, f32[2048,640]{0,1:T(8,128)}) fusion(bf16[2048,5120]{1,0:T(8,128)(2,1)} %bitcast.60, bf16[5120,640]{1,0:T(8,128)(2,1)} %param.15), kind=kOutput, calls=%fused_computation.13 | convolution fusion | flops 13424392192 | bytes 32776192 | tf_op jit(solution)/shard_map/dot_general | solution.py:96
  52.2 25.4 %all-reduce = (f32[2048]{0:T(1024)S(1)}, f32[2048]{0:T(1024)S(1)}) all-reduce(f32[2048]{0:T(1024)S(1)} %get-tuple-element.30, f32[2048]{0:T(1024)S(1)} %get-tuple-element.32), channel_id=1, replica_groups=mesh['dp'=1,'tp'=8] {'tp'}, use_global_device_ids=true, to_apply=%region_1.0 | all-reduce | flops 4096 | bytes 32768 | tf_op jit(solution)/shard_map/psum | solution.py:99
  140.3 18.3 %reduce-scatter.9.cloned.1.call-done = bf16[64,5120]{1,0:T(8,128)(2,1)} async-done(((bf16[512,5120]{1,0:T(8,128)(2,1)}), bf16[64,5120]{1,0:T(8,128)(2,1)}) %reduce-scatter.9.cloned.1.call-update) | async-done | bytes 655376 | tf_op jit(solution)/shard_map/reduce_scatter | solution.py:113
  162.4 47.1 %reduce-scatter.13.cloned.1.call-done = bf16[64,5120]{1,0:T(8,128)(2,1)} async-done(((bf16[512,5120]{1,0:T(8,128)(2,1)}), bf16[64,5120]{1,0:T(8,128)(2,1)}) %reduce-scatter.13.cloned.1.call-update) | async-done | bytes 655376 | tf_op jit(solution)/shard_map/reduce_scatter | solution.py:113
  213.4 47.2 %reduce-scatter.17.cloned.1.call-done = bf16[64,5120]{1,0:T(8,128)(2,1)} async-done(((bf16[512,5120]{1,0:T(8,128)(2,1)}), bf16[64,5120]{1,0:T(8,128)(2,1)}) %reduce-scatter.17.cloned.1.call-update) | async-done | bytes 655376 | tf_op jit(solution)/shard_map/reduce_scatter | solution.py:113
  264.4 47.6 %reduce-scatter.21.cloned.1.call-done = bf16[64,5120]{1,0:T(8,128)(2,1)} async-done(((bf16[512,5120]{1,0:T(8,128)(2,1)}), bf16[64,5120]{1,0:T(8,128)(2,1)}) %reduce-scatter.21.cloned.1.call-update) | async-done | bytes 655376 | tf_op jit(solution)/shard_map/reduce_scatter | solution.py:113
  315.9 33.0 %all-gather.9.cloned.1.call-done = bf16[512,5120]{1,0:T(8,128)(2,1)} async-done(((bf16[64,5120]{1,0:T(8,128)(2,1)}), bf16[512,5120]{1,0:T(8,128)(2,1)}) %all-gather.9.cloned.1.call-update) | async-done | bytes 5242896 | tf_op jit(solution)/shard_map/all_gather | solution.py:118
  348.8 26.7 %fusion.47 = f32[512,3456]{1,0:T(8,128)} fusion(bf16[512,5120]{1,0:T(8,128)(2,1)} %all-gather.9.cloned.1.call-done, bf16[5120,3456]{1,0:T(8,128)(2,1)} %param.23), kind=kOutput, calls=%fused_computation.93 | convolution fusion | flops 18119393280 | bytes 47710208 | tf_op jit(solution)/shard_map/dot_general | solution.py:121
  375.5 26.2 %multiply_convert_fusion.3.clone.2 = bf16[512,3456]{1,0:T(8,128)(2,1)S(1)} fusion(f32[512,3456]{1,0:T(8,128)} %fusion.47, bf16[512,5120]{1,0:T(8,128)(2,1)S(1)} %copy-done.8, bf16[5120,3456]{1,0:T(8,128)(2,1)} %param.24), kind=kOutput, calls=%fused_computation.12.clone.clone.clone | convolution fusion | flops 18130010112 | bytes 51249152 | tf_op jit(solution)/shard_map/dot_general | solution.py:122
  401.7 24.5 %convolution_convert_fusion.6 = bf16[512,5120]{1,0:T(8,128)(2,1)} fusion(bf16[3456,5120]{1,0:T(8,128)(2,1)} %param.25, bf16[512,3456]{1,0:T(8,128)(2,1)S(1)} %multiply_convert_fusion.3.clone.2), kind=kOutput, calls=%fused_computation.7 | convolution fusion | flops 18122014720 | bytes 44171264 | tf_op jit(solution)/shard_map/dot_general | solution.py:124
  426.5 26.7 %fusion.48 = f32[512,3456]{1,0:T(8,128)} fusion(bf16[512,5120]{1,0:T(8,128)(2,1)} %all-gather.13.cloned.1.call-done, bf16[5120,3456]{1,0:T(8,128)(2,1)} %param.23), kind=kOutput, calls=%fused_computation.94 | convolution fusion | flops 18119393280 | bytes 47710208 | tf_op jit(solution)/shard_map/dot_general | solution.py:121
  453.2 26.2 %multiply_convert_fusion.2.clone.2 = bf16[512,3456]{1,0:T(8,128)(2,1)S(1)} fusion(f32[512,3456]{1,0:T(8,128)} %fusion.48, bf16[512,5120]{1,0:T(8,128)(2,1)S(1)} %copy-done.9, bf16[5120,3456]{1,0:T(8,128)(2,1)} %param.24), kind=kOutput, calls=%fused_computation.11.clone.clone.clone | convolution fusion | flops 18130010112 | bytes 51249152 | tf_op jit(solution)/shard_map/dot_general | solution.py:122
  479.3 24.5 %convolution_convert_fusion.4 = bf16[512,5120]{1,0:T(8,128)(2,1)} fusion(bf16[3456,5120]{1,0:T(8,128)(2,1)} %param.25, bf16[512,3456]{1,0:T(8,128)(2,1)S(1)} %multiply_convert_fusion.2.clone.2), kind=kOutput, calls=%fused_computation.5 | convolution fusion | flops 18122014720 | bytes 44171264 | tf_op jit(solution)/shard_map/dot_general | solution.py:124
  504.1 26.7 %fusion.49 = f32[512,3456]{1,0:T(8,128)} fusion(bf16[512,5120]{1,0:T(8,128)(2,1)} %all-gather.17.cloned.1.call-done, bf16[5120,3456]{1,0:T(8,128)(2,1)} %param.23), kind=kOutput, calls=%fused_computation.95 | convolution fusion | flops 18119393280 | bytes 47710208 | tf_op jit(solution)/shard_map/dot_general | solution.py:121
  530.8 26.2 %multiply_convert_fusion.1.clone.2 = bf16[512,3456]{1,0:T(8,128)(2,1)S(1)} fusion(f32[512,3456]{1,0:T(8,128)} %fusion.49, bf16[512,5120]{1,0:T(8,128)(2,1)S(1)} %copy-done.10, bf16[5120,3456]{1,0:T(8,128)(2,1)} %param.24), kind=kOutput, calls=%fused_computation.10.clone.clone.clone | convolution fusion | flops 18130010112 | bytes 51249152 | tf_op jit(solution)/shard_map/dot_general | solution.py:122
  557.0 24.5 %convolution_convert_fusion.2 = bf16[512,5120]{1,0:T(8,128)(2,1)} fusion(bf16[3456,5120]{1,0:T(8,128)(2,1)} %param.25, bf16[512,3456]{1,0:T(8,128)(2,1)S(1)} %multiply_convert_fusion.1.clone.2), kind=kOutput, calls=%fused_computation.3 | convolution fusion | flops 18122014720 | bytes 44171264 | tf_op jit(solution)/shard_map/dot_general | solution.py:124
  581.8 26.7 %fusion.50 = f32[512,3456]{1,0:T(8,128)} fusion(bf16[512,5120]{1,0:T(8,128)(2,1)} %all-gather.21.cloned.1.call-done, bf16[5120,3456]{1,0:T(8,128)(2,1)} %param.23), kind=kOutput, calls=%fused_computation.96 | convolution fusion | flops 18119393280 | bytes 47710208 | tf_op jit(solution)/shard_map/dot_general | solution.py:121
  608.5 26.2 %multiply_convert_fusion.clone.4 = bf16[512,3456]{1,0:T(8,128)(2,1)S(1)} fusion(f32[512,3456]{1,0:T(8,128)} %fusion.50, bf16[512,5120]{1,0:T(8,128)(2,1)S(1)} %copy-done.11, bf16[5120,3456]{1,0:T(8,128)(2,1)} %param.24), kind=kOutput, calls=%fused_computation.9.clone.clone.clone.1 | convolution fusion | flops 18130010112 | bytes 51249152 | tf_op jit(solution)/shard_map/dot_general | solution.py:122
  634.7 24.4 %convolution_convert_fusion = bf16[512,5120]{1,0:T(8,128)(2,1)} fusion(bf16[3456,5120]{1,0:T(8,128)(2,1)} %param.25, bf16[512,3456]{1,0:T(8,128)(2,1)S(1)} %multiply_convert_fusion.clone.4), kind=kOutput, calls=%fused_computation.1 | convolution fusion | flops 18122014720 | bytes 44171264 | tf_op jit(solution)/shard_map/dot_general | solution.py:124
  670.9 36.1 %reduce-scatter.23.cloned.1.call-done = bf16[64,5120]{1,0:T(8,128)(2,1)} async-done(((bf16[512,5120]{1,0:T(8,128)(2,1)}), bf16[64,5120]{1,0:T(8,128)(2,1)}) %reduce-scatter.23.cloned.1.call-update) | async-done | bytes 655376 | tf_op jit(solution)/shard_map/reduce_scatter | solution.py:125
  710.6 33.4 %all-gather.11.cloned.1.call-done = bf16[512,5120]{1,0:T(8,128)(2,1)} async-done(((bf16[64,5120]{1,0:T(8,128)(2,1)}), bf16[512,5120]{1,0:T(8,128)(2,1)}) %all-gather.11.cloned.1.call-update) | async-done | bytes 5242896 | tf_op jit(solution)/shard_map/all_gather | solution.py:129
  744.0 36.8 %all-gather.15.cloned.1.call-done = bf16[512,5120]{1,0:T(8,128)(2,1)} async-done(((bf16[64,5120]{1,0:T(8,128)(2,1)}), bf16[512,5120]{1,0:T(8,128)(2,1)}) %all-gather.15.cloned.1.call-update) | async-done | bytes 5242896 | tf_op jit(solution)/shard_map/all_gather | solution.py:129
  780.8 36.8 %all-gather.19.cloned.1.call-done = bf16[512,5120]{1,0:T(8,128)(2,1)} async-done(((bf16[64,5120]{1,0:T(8,128)(2,1)}), bf16[512,5120]{1,0:T(8,128)(2,1)}) %all-gather.19.cloned.1.call-update) | async-done | bytes 5242896 | tf_op jit(solution)/shard_map/all_gather | solution.py:129
  817.6 37.4 %all-gather.23.cloned.1.call-done = bf16[512,5120]{1,0:T(8,128)(2,1)} async-done(((bf16[64,5120]{1,0:T(8,128)(2,1)}), bf16[512,5120]{1,0:T(8,128)(2,1)}) %all-gather.23.cloned.1.call-update) | async-done | bytes 5242896 | tf_op jit(solution)/shard_map/all_gather | solution.py:129
  (105 shorter events, 136.0 us)
Async XLA Ops:
  7.2 12.5 %copy-start = (bf16[5120,128]{1,0:T(8,128)(2,1)S(1)}, bf16[5120,128]{1,0:T(8,128)(2,1)}, u32[]{:S(2)}) copy-start(bf16[5120,128]{1,0:T(8,128)(2,1)} %param.16) | copy-start | bytes 3932164
  7.2 151.4 %reduce-scatter.9.cloned.1.call-start = ((), (), s32[]{:S(2)}) async-start(), calls=%async_computation.8 | async-start | bytes 5898240 | tf_op jit(solution)/shard_map/reduce_scatter | solution.py:113
  109.9 99.7 %reduce-scatter.13.cloned.1.call-start = ((), (), s32[]{:S(2)}) async-start(), calls=%async_computation.12 | async-start | bytes 5898240 | tf_op jit(solution)/shard_map/reduce_scatter | solution.py:113
  119.6 140.9 %reduce-scatter.17.cloned.1.call-start = ((), (), s32[]{:S(2)}) async-start(), calls=%async_computation.16 | async-start | bytes 5898240 | tf_op jit(solution)/shard_map/reduce_scatter | solution.py:113
  129.4 182.6 %reduce-scatter.21.cloned.1.call-start = ((), (), s32[]{:S(2)}) async-start(), calls=%async_computation.20 | async-start | bytes 5898240 | tf_op jit(solution)/shard_map/reduce_scatter | solution.py:113
  139.6 209.3 %all-gather.9.cloned.1.call-start = ((), (), s32[]{:S(2)}) async-start(), calls=%async_computation.9 | async-start | bytes 5898240 | tf_op jit(solution)/shard_map/all_gather | solution.py:118
  162.4 264.1 %all-gather.13.cloned.1.call-start = ((), (), s32[]{:S(2)}) async-start(), calls=%async_computation.13 | async-start | bytes 5898240 | tf_op jit(solution)/shard_map/all_gather | solution.py:118
  213.3 290.8 %all-gather.17.cloned.1.call-start = ((), (), s32[]{:S(2)}) async-start(), calls=%async_computation.17 | async-start | bytes 5898240 | tf_op jit(solution)/shard_map/all_gather | solution.py:118
  264.4 317.4 %all-gather.21.cloned.1.call-start = ((), (), s32[]{:S(2)}) async-start(), calls=%async_computation.21 | async-start | bytes 5898240 | tf_op jit(solution)/shard_map/all_gather | solution.py:118
  315.8 344.0 %reduce-scatter.11.cloned.1.call-start = ((), (), s32[]{:S(2)}) async-start(), calls=%async_computation.10 | async-start | bytes 5898240 | tf_op jit(solution)/shard_map/reduce_scatter | solution.py:125
  348.8 26.7 %copy-start.8 = (bf16[512,5120]{1,0:T(8,128)(2,1)S(1)}, bf16[512,5120]{1,0:T(8,128)(2,1)}, u32[]{:S(2)}) copy-start(bf16[512,5120]{1,0:T(8,128)(2,1)} %all-gather.9.cloned.1.call-done) | copy-start | bytes 15728644
  426.2 237.3 %reduce-scatter.15.cloned.1.call-start = ((), (), s32[]{:S(2)}) async-start(), calls=%async_computation.14 | async-start | bytes 5898240 | tf_op jit(solution)/shard_map/reduce_scatter | solution.py:125
  426.5 26.7 %copy-start.9 = (bf16[512,5120]{1,0:T(8,128)(2,1)S(1)}, bf16[512,5120]{1,0:T(8,128)(2,1)}, u32[]{:S(2)}) copy-start(bf16[512,5120]{1,0:T(8,128)(2,1)} %all-gather.13.cloned.1.call-done) | copy-start | bytes 15728644
  503.8 163.4 %reduce-scatter.19.cloned.1.call-start = ((), (), s32[]{:S(2)}) async-start(), calls=%async_computation.18 | async-start | bytes 5898240 | tf_op jit(solution)/shard_map/reduce_scatter | solution.py:125
  504.1 26.7 %copy-start.10 = (bf16[512,5120]{1,0:T(8,128)(2,1)S(1)}, bf16[512,5120]{1,0:T(8,128)(2,1)}, u32[]{:S(2)}) copy-start(bf16[512,5120]{1,0:T(8,128)(2,1)} %all-gather.17.cloned.1.call-done) | copy-start | bytes 15728644
  581.5 125.5 %reduce-scatter.23.cloned.1.call-start = ((), (), s32[]{:S(2)}) async-start(), calls=%async_computation.22 | async-start | bytes 5898240 | tf_op jit(solution)/shard_map/reduce_scatter | solution.py:125
  581.8 26.7 %copy-start.11 = (bf16[512,5120]{1,0:T(8,128)(2,1)S(1)}, bf16[512,5120]{1,0:T(8,128)(2,1)}, u32[]{:S(2)}) copy-start(bf16[512,5120]{1,0:T(8,128)(2,1)} %all-gather.21.cloned.1.call-done) | copy-start | bytes 15728644
  659.1 9.5 %copy-start.4 = (bf16[64,5120]{1,0:T(8,128)(2,1)S(1)}, bf16[64,5120]{1,0:T(8,128)(2,1)}, u32[]{:S(2)}) copy-start(bf16[64,5120]{1,0:T(8,128)(2,1)} %fusion.23) | copy-start | bytes 1966084
  659.1 84.8 %all-gather.11.cloned.1.call-start = ((), (), s32[]{:S(2)}) async-start(), calls=%async_computation.11 | async-start | bytes 5898240 | tf_op jit(solution)/shard_map/all_gather | solution.py:129
  659.8 48.5 %copy-start.5 = (bf16[64,5120]{1,0:T(8,128)(2,1)S(1)}, bf16[64,5120]{1,0:T(8,128)(2,1)}, u32[]{:S(2)}) copy-start(bf16[64,5120]{1,0:T(8,128)(2,1)} %fusion.31) | copy-start | bytes 1966084
  663.5 117.3 %all-gather.15.cloned.1.call-start = ((), (), s32[]{:S(2)}) async-start(), calls=%async_computation.15 | async-start | bytes 5898240 | tf_op jit(solution)/shard_map/all_gather | solution.py:129
  667.2 150.5 %all-gather.19.cloned.1.call-start = ((), (), s32[]{:S(2)}) async-start(), calls=%async_computation.19 | async-start | bytes 5898240 | tf_op jit(solution)/shard_map/all_gather | solution.py:129
  670.9 184.2 %all-gather.23.cloned.1.call-start = ((), (), s32[]{:S(2)}) async-start(), calls=%async_computation.23 | async-start | bytes 5898240 | tf_op jit(solution)/shard_map/all_gather | solution.py:129
  855.0 17.0 %copy-start.1 = (bf16[5120,128]{1,0:T(8,128)(2,1)S(1)}, bf16[5120,128]{1,0:T(8,128)(2,1)}, u32[]{:S(2)}) copy-start(bf16[5120,128]{1,0:T(8,128)(2,1)} %param.16) | copy-start | bytes 3932164
  (4 other events, 9.3 us)
Sparse Core Ops, SparseCore 0:
  110.0 48.5 reduce-scatter.8
  161.9 47.6 reduce-scatter.12
  212.9 47.6 reduce-scatter.16
  264.3 47.6 reduce-scatter.20
  313.7 35.1 all-gather.8
  350.5 35.1 all-gather.12
  387.5 35.1 all-gather.16
  424.5 35.1 all-gather.20
  463.0 47.6 reduce-scatter.10
  513.9 47.6 reduce-scatter.14
  581.6 47.6 reduce-scatter.18
  659.3 47.6 reduce-scatter.22
  708.8 35.1 all-gather.10
  745.6 35.1 all-gather.14
  782.5 35.1 all-gather.18
  819.9 35.1 all-gather.22

commit v2 on v1

--- a/solution.py
+++ b/solution.py
@@ -1,3 +1,5 @@
+import functools
+
 import jax
 import jax.numpy as jnp
 from jax import lax
@@ -71,7 +73,6 @@
         return pl.BlockSpec((rows, w), lambda i, lens: (i, 0))
     def full(shape):
         return pl.BlockSpec(shape, lambda i, lens: (0, 0))
-    import functools
     return pl.pallas_call(
         functools.partial(attn_kernel, seq_len, group, per_step),
         grid_spec=pltpu.PrefetchScalarGridSpec(
@@ -85,13 +86,226 @@
     )(seq_lens, q_raw, k_raw, v, inv_q, inv_k, g_q[None], g_k[None], cos, sin)
 
 
+MESH = pl.DeviceIdType.MESH
+GU = 384
+DN = 512
+BLK = 16
+
+
+def layer_kernel(chunks, x_ref, o_ref, wo_ref, wg_ref, wu_ref, wd_ref, ga_ref, gm_ref, y_ref,
+                 wgu, wdb, wob, h, act, part, r0, r1, r2, obuf, xo, ho, yo,
+                 gu_sem, wd_sem, wo_sem, o_sem, xo_sem, yo_sem, send, recv):
+    size, width = part.shape
+    gu_tiles = wg_ref.shape[1] // GU
+    dn_tiles = width // DN
+    steps = gu_tiles + dn_tiles
+    me = lax.axis_index('tp')
+    core = lax.rem(me, 2)
+    xi = lax.rem(lax.div(me, 2), 2)
+    yi = lax.div(me, 4)
+    core_dev, x_dev, y_dev = me + 1 - 2 * core, me + 2 - 4 * xi, me + 4 - 8 * yi
+    half = size // 2
+    n0, n1, n2 = half // 2, half // 4, half // 8
+    first, second = (xi, yi), (yi, xi)
+    first_dev, second_dev = (x_dev, y_dev), (y_dev, x_dev)
+
+    barrier = pltpu.get_barrier_semaphore()
+    for dev in (core_dev, x_dev, y_dev):
+        pl.semaphore_signal(barrier, inc=1, device_id={'tp': dev}, device_id_type=MESH)
+    pl.semaphore_wait(barrier, 3)
+
+    def rows(start, count):
+        return pl.ds(pl.multiple_of(start, n2), count)
+
+    def remote(stream, phase, col, chunk):
+        base = col * half
+        p = pl.multiple_of(base + core * n0, n0)
+        q = pl.multiple_of(p + first[col] * n1, n1)
+        own = pl.multiple_of(q + second[col] * n2, n2)
+        if phase == 0:
+            src, dst, dev = part.at[rows(base + (1 - core) * n0, n0)], r0.at[stream, pl.ds(col * n0, n0)], core_dev
+        elif phase == 1:
+            src, dst, dev = r0.at[stream, rows(col * n0 + (1 - first[col]) * n1, n1)], r1.at[stream, pl.ds(col * n1, n1)], first_dev[col]
+        elif phase == 2:
+            src, dst, dev = r1.at[stream, rows(col * n1 + (1 - second[col]) * n2, n2)], r2.at[stream, pl.ds(col * n2, n2)], second_dev[col]
+        else:
+            start, count, dev = ((own, n2, second_dev[col]), (q, n1, first_dev[col]), (p, n0, core_dev))[phase - 3]
+            if stream == 0:
+                src = dst = h.at[lax.rem(chunk, 2), rows(start, count)]
+            else:
+                dst = y_ref.at[rows(chunk * size + start, count)]
+                src = yo.at[pl.ds(col * n2, n2)] if phase == 3 else dst
+        return pltpu.make_async_remote_copy(src_ref=src, dst_ref=dst, send_sem=send.at[stream, phase, col], recv_sem=recv.at[stream, phase, col], device_id={'tp': dev}, device_id_type=MESH)
+
+    def own_row(col):
+        return col * half + core * n0 + first[col] * n1 + second[col] * n2
+
+    def x_copy(col, chunk):
+        return pltpu.make_async_copy(x_ref.at[rows(chunk * size + own_row(col), n2)], xo.at[pl.ds(col * n2, n2)], xo_sem.at[col])
+
+    def y_copy(col, chunk):
+        return pltpu.make_async_copy(yo.at[pl.ds(col * n2, n2)], y_ref.at[rows(chunk * size + own_row(col), n2)], yo_sem.at[col])
+
+    def o_copy(chunk):
+        return pltpu.make_async_copy(o_ref.at[rows(chunk * size, size)], obuf, o_sem)
+
+    def gu_copies(chunk, j):
+        slot = lax.rem(chunk * gu_tiles + j, 2)
+        cols = pl.ds(pl.multiple_of(j * GU, GU), GU)
+        return (pltpu.make_async_copy(wg_ref.at[:, cols], wgu.at[slot, :, pl.ds(0, GU)], gu_sem.at[slot, 0]),
+                pltpu.make_async_copy(wu_ref.at[:, cols], wgu.at[slot, :, pl.ds(GU, GU)], gu_sem.at[slot, 1]))
+
+    def dn_copy(k):
+        slot = lax.rem(k, 2)
+        return pltpu.make_async_copy(wd_ref.at[:, pl.ds(pl.multiple_of(k * DN, DN), DN)], wdb.at[slot], wd_sem.at[slot])
+
+    def add_into(dst, dst_start, src, src_start, count):
+        @pl.loop(0, count // BLK)
+        def _(i):
+            d = pl.ds(pl.multiple_of(dst_start + i * BLK, BLK), BLK)
+            s = pl.ds(pl.multiple_of(src_start + i * BLK, BLK), BLK)
+            dst[d, :] = (dst[d, :].astype(jnp.float32) + src[s, :].astype(jnp.float32)).astype(jnp.bfloat16)
+
+    def project(chunk):
+        o_copy(chunk).wait()
+
+        @pl.loop(0, dn_tiles)
+        def _(k):
+            cols = pl.ds(pl.multiple_of(k * DN, DN), DN)
+            part[:, cols] = jnp.dot(obuf[...], wob[:, cols], preferred_element_type=jnp.float32).astype(jnp.bfloat16)
+
+    def event(stream, e, chunk):
+        for col in range(2):
+            if e == 0:
+                remote(stream, 0, col, chunk).start()
+                continue
+            prev = remote(stream, e - 1, col, chunk)
+            prev.wait_recv()
+            prev.wait_send()
+            if e == 1:
+                add_into(r0.at[stream], col * n0, part, col * half + core * n0, n0)
+            elif e == 2:
+                add_into(r1.at[stream], col * n1, r0.at[stream], col * n0 + first[col] * n1, n1)
+                if stream == 0:
+                    x_copy(col, chunk).start()
+            elif e == 3:
+                gain = ga_ref if stream == 0 else gm_ref
+                par = lax.rem(chunk, 2)
+                if stream == 0:
+                    x_copy(col, chunk).wait()
+
+                @pl.loop(0, n2 // BLK)
+                def _(i):
+                    mine = pl.ds(pl.multiple_of(col * n2 + i * BLK, BLK), BLK)
+                    kept = pl.ds(pl.multiple_of(col * n1 + second[col] * n2 + i * BLK, BLK), BLK)
+                    total = (r2[stream, mine, :].astype(jnp.float32) + r1[stream, kept, :].astype(jnp.float32)).astype(jnp.bfloat16)
+                    base = xo[mine, :] if stream == 0 else ho[par, mine, :]
+                    out = post_norm(base, total, gain[...])
+                    if stream == 0:
+                        h[par, pl.ds(pl.multiple_of(own_row(col) + i * BLK, BLK), BLK), :] = out
+                        ho[par, mine, :] = out
+                    else:
+                        yo[mine, :] = out
+                if stream == 1:
+                    y_copy(col, chunk).start()
+            elif e == 4 and stream == 1:
+                y_copy(col, chunk).wait()
+            if e < 6:
+                remote(stream, e, col, chunk).start()
+
+    pltpu.make_async_copy(wo_ref, wob, wo_sem).start()
+    o_copy(0).start()
+    for cp in gu_copies(0, 0):
+        cp.start()
+    dn_copy(0).start()
+    pltpu.make_async_copy(wo_ref, wob, wo_sem).wait()
+
+    points = {(1, 1): 1, (1, 2): 4, (1, 3): 6, (1, 4): 8, (1, 5): 11, (1, 6): 15,
+              (0, 0): 1, (0, 1): 2, (0, 2): 5, (0, 3): 7, (0, 4): 10, (0, 5): 14, (0, 6): 18}
+
+    @pl.loop(0, chunks + 2)
+    def _(it):
+        c = it - 1
+        computes = (it >= 1) & (it <= chunks)
+
+        @pl.loop(0, steps)
+        def _(j):
+            for (stream, e), at in sorted(points.items(), key=lambda kv: (kv[1], -kv[0][0])):
+                live = (it < chunks) if stream == 0 else (it >= 2)
+
+                @pl.when((j == at) & live)
+                def _():
+                    chunk = it if stream == 0 else it - 2
+                    if (stream, e) == (0, 0):
+                        project(chunk)
+
+                        @pl.when(it + 1 < chunks)
+                        def _():
+                            o_copy(chunk + 1).start()
+                    event(stream, e, chunk)
+
+            @pl.when(computes & (j < gu_tiles))
+            def _():
+                for cp in gu_copies(c, j):
+                    cp.wait()
+
+                @pl.when((j + 1 < gu_tiles) | (it < chunks))
+                def _():
+                    wraps = (j + 1 >= gu_tiles).astype(jnp.int32)
+                    for cp in gu_copies(c + wraps, (j + 1) * (1 - wraps)):
+                        cp.start()
+                slot = lax.rem(c * gu_tiles + j, 2)
+                both = jnp.dot(h[lax.rem(c, 2)], wgu[slot], preferred_element_type=jnp.float32)
+                gate, up = both[:, :GU], both[:, GU:]
+                act[:, pl.ds(pl.multiple_of(j * GU, GU), GU)] = (gate * lax.logistic(gate) * up).astype(jnp.bfloat16)
+
+            @pl.when(computes & (j >= gu_tiles))
+            def _():
+                k = j - gu_tiles
+                dn_copy(k).wait()
+
+                @pl.when((k + 1 < dn_tiles) | (it < chunks))
+                def _():
+                    wraps = (k + 1 >= dn_tiles).astype(jnp.int32)
+                    dn_copy((k + 1) * (1 - wraps)).start()
+                part[:, pl.ds(pl.multiple_of(k * DN, DN), DN)] = jnp.dot(act[...], wdb[lax.rem(k, 2)], preferred_element_type=jnp.float32).astype(jnp.bfloat16)
+
+        @pl.when(computes)
+        def _():
+            event(1, 0, c)
+
+
+def layer_tail(x, o, w_o, w_gate, w_up, w_down, g_attn, g_mlp):
+    tokens, width = x.shape
+    size = tokens // CHUNKS
+    inner = w_gate.shape[1]
+    bf = jnp.bfloat16
+    anyspec = pl.BlockSpec(memory_space=pl.ANY)
+    vmem = pl.BlockSpec(memory_space=pltpu.VMEM)
+    dma = pltpu.SemaphoreType.DMA
+    return pl.pallas_call(
+        functools.partial(layer_kernel, CHUNKS),
+        out_shape=jax.ShapeDtypeStruct((tokens, width), bf),
+        in_specs=[anyspec] * 6 + [vmem] * 2,
+        out_specs=anyspec,
+        scratch_shapes=[
+            pltpu.VMEM((2, width, 2 * GU), bf), pltpu.VMEM((2, inner, DN), bf), pltpu.VMEM(w_o.shape, bf),
+            pltpu.VMEM((2, size, width), bf), pltpu.VMEM((size, inner), bf), pltpu.VMEM((size, width), bf),
+            pltpu.VMEM((2, size // 2, width), bf), pltpu.VMEM((2, size // 4, width), bf), pltpu.VMEM((2, size // 8, width), bf),
+            pltpu.VMEM((size, o.shape[1]), bf), pltpu.VMEM((size // 8, width), bf), pltpu.VMEM((2, size // 8, width), bf), pltpu.VMEM((size // 8, width), bf),
+            dma((2, 2)), dma((2,)), dma, dma, dma((2,)), dma((2,)), dma((2, 6, 2)), dma((2, 6, 2)),
+        ],
+        compiler_params=pltpu.CompilerParams(collective_id=0, has_side_effects=True, vmem_limit_bytes=67043328),
+        cost_estimate=pl.CostEstimate(flops=2 * tokens * width * (3 * inner + o.shape[1]), bytes_accessed=CHUNKS * 3 * inner * width * 2, transcendentals=tokens * inner),
+    )(x, o, w_o, w_gate, w_up, w_down, g_attn[None], g_mlp[None])
+
+
 def solution(mesh):
     tp_size = mesh.shape['tp']
 
     def local_layer(tokens, seq_lens, w_q, w_k, w_v, w_o, g_q, g_k, g_attn, g_mlp, w_gate, w_up, w_down):
         prompts, seq_len, width = tokens.shape
         x = tokens.reshape(prompts * seq_len, width)
-        me = lax.axis_index('tp')
         f32 = dict(preferred_element_type=jnp.float32)
         q_raw = jnp.dot(x, w_q, **f32)
         k_raw = jnp.dot(x, w_k, **f32)
@@ -104,30 +318,7 @@
         k_cache = keys.reshape(prompts, 1, seq_len, HEAD_DIM)
         v_cache = v.reshape(prompts, 1, seq_len, HEAD_DIM)
 
-        size = prompts * seq_len // CHUNKS
-        own = size // tp_size
-        outs = []
-        hs = []
-        for c in range(CHUNKS):
-            part = jnp.dot(lax.slice_in_dim(o, c * size, (c + 1) * size), w_o, **f32).astype(jnp.bfloat16)
-            a_own = lax.psum_scatter(part, 'tp', scatter_dimension=0, tiled=True)
-            if hs:
-                a_own, _ = lax.optimization_barrier((a_own, hs[-1][0]))
-            x_own = lax.dynamic_slice_in_dim(x, c * size + me * own, own)
-            h_own = post_norm(x_own, a_own, g_attn)
-            hs.append((h_own, lax.all_gather(h_own, 'tp', axis=0, tiled=True)))
-        for c in range(CHUNKS):
-            h_own, h = hs[c]
-            gate = jnp.dot(h, w_gate, **f32)
-            up = jnp.dot(h, w_up, **f32)
-            act = (jax.nn.silu(gate) * up).astype(jnp.bfloat16)
-            part = jnp.dot(act, w_down, **f32).astype(jnp.bfloat16)
-            m_own = lax.psum_scatter(part, 'tp', scatter_dimension=0, tiled=True)
-            if outs:
-                m_own, _ = lax.optimization_barrier((m_own, y_own))
-            y_own = post_norm(h_own, m_own, g_mlp)
-            outs.append(lax.all_gather(y_own, 'tp', axis=0, tiled=True))
-        y = jnp.concatenate(outs, axis=0).reshape(prompts, seq_len, width)
+        y = layer_tail(x, o, w_o, w_gate, w_up, w_down, g_attn, g_mlp).reshape(prompts, seq_len, width)
         return y, k_cache, v_cache
 
     return jax.shard_map(local_layer, mesh=mesh, in_specs=(P('dp', None, None), P('dp'), P(None, 'tp'), P(None, 'tp'), P(None, 'tp'), P('tp', None), P('tp'), P('tp'), P(), P(), P(None, 'tp'), P(None, 'tp'), P('tp', None)), out_specs=(P('dp', None, None), P('dp', 'tp', None, None), P('dp', 'tp', None, None)), check_vma=False)

time: 886 us -> 597 us (0.67)
  Pallas kernels: 13.2 us -> 496 us
  waiting for transfers between devices: 374 us -> 0 us
  matrix products: 390 us -> 42.2 us
  other arithmetic: 47.2 us -> 0.88 us
  local copies, waits for them, and re-layouts: 12.7 us -> 31.5 us
  between operations: 14.7 us -> 0.66 us
    pallas_call x0 -> x1, Pallas kernels: none -> 482 us  [layer_tail(): pl.pallas_call(functools.partial(layer_kernel, CHUNKS), out_shape=jax.Sha...]
    dot_general x16 -> x0, matrix products: 348 us -> none  [the longest x4 107 us: local_layer(): gate = jnp.dot(h, w_gate, **f32)]
    reduce_scatter x8 -> x0, waiting for transfers between devices: 196 us -> none  [the longest x4 160 us: local_layer(): a_own = lax.psum_scatter(part, 'tp', scatter_dimension=0, tiled=True)]
    all_gather x8 -> x0, waiting for transfers between devices: 178 us -> none  [the longest x4 144 us: local_layer(): outs.append(lax.all_gather(y_own, 'tp', axis=0, tiled=True))]
    convert_element_type x10 -> x0, other arithmetic: 18.7 us -> none  [the longest x8 18.7 us: post_norm(): (base.astype(jnp.float32) + branch32 * rms_scale(branch32) * gain.astype(...]
    concatenate x1 -> x0, other arithmetic: 17 us -> none  [local_layer(): y = jnp.concatenate(outs, axis=0).reshape(prompts, seq_len, width)]
    unnamed x24 -> x3, local copies, waits for them, and re-layouts: 1.29 us -> 17.6 us
    reduce_sum x8 -> x0, other arithmetic: 10.6 us -> none  [rms_scale(): return lax.rsqrt(jnp.mean(vals * vals, axis=-1, keepdims=True) + NORM_EPS)]
  transfers between devices with their start and end apart: 16 -> 0, of which waited for: 10 -> 0; matrix products, arithmetic and copies ran while one was open for 42% -> 0% of each run, Pallas kernels for 0% -> 0%
where the time goes in v2:
time: 597 us; the launch traced here: 596 us
  Pallas kernels  496 us (83%)
  matrix products  42.2 us (7%)
  local copies, waits for them, and re-layouts  31.5 us (5%)
  blocking collectives  25.4 us (4%)
    pallas_call x1, Pallas kernels, layer_tail(): pl.pallas_call(functools.partial(layer_kernel, CHUNKS), out_shape=jax.Sha...  482 us
    psum x1, blocking collectives, local_layer(): lax.psum((jnp.sum(q_raw * q_raw, axis=-1), jnp.sum(k_raw * k_raw, axis=-1...  25.4 us
    dot_general x1, matrix products, local_layer(): q_raw = jnp.dot(x, w_q, **f32)  19.9 us
    unnamed x3, local copies, waits for them, and re-layouts  17.6 us
    pallas_call x1, Pallas kernels, attention(): pl.pallas_call(functools.partial(attn_kernel, seq_len, group, per_step),...  13.2 us

profile of v2, /device:TPU:0, one launch (start us, length us, event | category | flops | bytes accessed | tf_op | source)
XLA Modules:
  0.0 596.1 jit_solution(15928432641623785029)
XLA Ops:
  0.6 1.3 broadcast_in_dim.22.gq_ref
  1.9 1.3 broadcast_in_dim.24.ga_ref
  3.2 1.3 broadcast_in_dim.25.gm_ref
  4.6 0.1 fusion.2
  4.7 0.7 pad_maximum_fusion
  5.4 0.0 copy-start
  5.4 11.0 %convolution_convert_fusion.v_ref = bf16[2048,128]{1,0:T(8,128)(2,1)} fusion(bf16[2048,5120]{1,0:T(8,128)(2,1)} %bitcast.17, bf16[5120,128]{1,0:T(8,128)(2,1)} %param.17), kind=kOutput, calls=%fused_computation.1 | convolution fusion | flops 2684616704 | bytes 22806528 | tf_op jit(solution)/shard_map/dot_general | solution.py:312
  16.4 0.0 copy-done
  16.4 11.3 %multiply_reduce_fusion.1 = (f32[2048]{0:T(1024)S(1)}, f32[2048,128]{0,1:T(8,128)S(1)}) fusion(bf16[2048,5120]{1,0:T(8,128)(2,1)} %bitcast.18, bf16[5120,128]{1,0:T(8,128)(2,1)S(1)} %copy-done), kind=kOutput, calls=%fused_computation.2 | convolution fusion | flops 2684876800 | bytes 23339008 | tf_op jit(solution)/shard_map/dot_general | solution.py:311
  27.7 1.4 copy.21.k_ref
  29.1 19.9 %multiply_reduce_fusion = (f32[2048]{0:T(1024)S(1)}, f32[2048,640]{0,1:T(8,128)}) fusion(bf16[2048,5120]{1,0:T(8,128)(2,1)} %bitcast.19, bf16[5120,640]{1,0:T(8,128)(2,1)} %param.15), kind=kOutput, calls=%fused_computation | convolution fusion | flops 13424392192 | bytes 32776192 | tf_op jit(solution)/shard_map/dot_general | solution.py:310
  49.0 25.4 %all-reduce = (f32[2048]{0:T(1024)S(1)}, f32[2048]{0:T(1024)S(1)}) all-reduce(f32[2048]{0:T(1024)S(1)} %get-tuple-element.18, f32[2048]{0:T(1024)S(1)} %get-tuple-element.20), channel_id=1, replica_groups=mesh['dp'=1,'tp'=8] {'tp'}, use_global_device_ids=true, to_apply=%region_1.0 | all-reduce | flops 4096 | bytes 32768 | tf_op jit(solution)/shard_map/psum | solution.py:313
  74.4 1.4 copy.22.iq_ref
  75.8 1.4 copy.23.ik_ref
  77.1 5.9 copy.20.q_ref
  83.0 13.2 %shard_map.148 = (bf16[2048,640]{1,0:T(8,128)(2,1)}, bf16[2048,128]{1,0:T(8,128)(2,1)}) custom-call(s32[32]{0:T(128)} %lens_ref.1, f32[2048,640]{1,0:T(8,128)} %copy.20.q_ref, f32[2048,128]{1,0:T(8,128)} %copy.21.k_ref, bf16[2048,128]{1,0:T(8,128)(2,1)} %convolution_convert_fusion.v_ref, f32[2048,1]{1,0:T(8,128)} %copy.22.iq_ref, f32[2048,1]{1,0:T(8,128)} %copy.23.ik_ref, ...), custom_call_target="tpu_custom_call" | custom-call | flops 335544320 | bytes 7864320 | tf_op jit(solution)/shard_map/pallas_call | solution.py:76
  96.3 482.3 %shard_map.149 = bf16[2048,5120]{1,0:T(8,128)(2,1)} custom-call(bf16[2048,5120]{1,0:T(8,128)(2,1)} %bitcast.20, bf16[2048,640]{1,0:T(8,128)(2,1)} %get-tuple-element.5.o_ref, bf16[640,5120]{1,0:T(8,128)(2,1)} %wo_ref.1, bf16[5120,3456]{1,0:T(8,128)(2,1)} %wg_ref.1, bf16[5120,3456]{1,0:T(8,128)(2,1)} %wu_ref.1, bf16[3456,5120]{1,0:T(8,128)(2,1)} %wd_ref.1, ...), custom_call_target="tpu_custom_call" | custom-call | flops 230854492160 | bytes 424673280 | tf_op jit(solution)/shard_map/pallas_call | solution.py:286
  578.5 17.5 %copy.27 = bf16[32,64,5120]{2,1,0:T(8,128)(2,1)} copy(bf16[32,64,5120]{2,1,0:T(8,128)(2,1)} %bitcast.21) | data formatting | bytes 41943040
  (2 shorter events, 0.0 us)
Async XLA Ops:
  5.4 11.0 %copy-start = (bf16[5120,128]{1,0:T(8,128)(2,1)S(1)}, bf16[5120,128]{1,0:T(8,128)(2,1)}, u32[]{:S(2)}) copy-start(bf16[5120,128]{1,0:T(8,128)(2,1)} %param.16) | copy-start | bytes 3932164

commit v3 on v0

v3 whole, which is shorter than its diff:
```python
import functools

import jax
import jax.numpy as jnp
import numpy as np
from jax import lax
from jax.experimental import pallas as pl
from jax.experimental.pallas import tpu as pltpu
from jax.sharding import PartitionSpec as P

HEAD_DIM = 128
ROPE_BASE = 500000.0
NORM_EPS = 1e-6
MESH = pl.DeviceIdType.MESH
CHUNKS = 4
GU = 384
DN = 512
BLK = 16
STAT = 128

PROLOGUE, STEPS = 19, 103
EVENTS = {
    (2, 0): (0, 3, 6, 13),
    (2, 1): (1, 5, 11, 16),
    (0, 6): (18, 29, 43, 60),
    (0, 5): (17, 27, 41, 59),
    (0, 4): (12, 22, 32, 51),
    (0, 3): (9, 20, 28, 47),
    (0, 2): (7, 14, 25, 38),
    (0, 1): (4, 10, 20, 28),
    (0, 0): (2, 8, 15, 25),
    (1, 6): (64, 79, 97, 102),
    (1, 5): (62, 78, 95, 101),
    (1, 4): (54, 71, 87, 100),
    (1, 3): (47, 66, 84, 99),
    (1, 2): (45, 64, 82, 98),
    (1, 1): (39, 59, 78, 96),
}


def rope_tables(seq_len, head_dim):
    half_dim = head_dim // 2
    inv_freq = np.float32(ROPE_BASE) ** (np.float32(-2.0) * np.arange(half_dim, dtype=np.float32) / np.float32(head_dim))
    angles = np.arange(seq_len, dtype=np.float32)[:, None] * inv_freq[None, :].astype(np.float32)
    cos, sin = np.cos(angles).astype(np.float32), np.sin(angles).astype(np.float32)
    return np.concatenate([cos, cos], axis=-1), np.concatenate([-sin, sin], axis=-1)


def rms_scale(vals):
    return lax.rsqrt(jnp.mean(vals * vals, axis=-1, keepdims=True) + NORM_EPS)


def post_norm(base, branch, gain):
    branch32 = branch.astype(jnp.float32)
    return (base.astype(jnp.float32) + branch32 * rms_scale(branch32) * gain.astype(jnp.float32)).astype(jnp.bfloat16)


def layer_kernel(seq_len, tp_size, lens_ref, x_ref, wq_ref, wk_ref, wv_ref, wo_ref, wg_ref, wu_ref, wd_ref,
                 gq_ref, gk_ref, ga_ref, gm_ref, cos_ref, sin_ref, y_ref, kc_ref, vc_ref,
                 wgu, wdb, h, act, part, r0, r1, r2, obuf, qk, ho, yo, stat, stat_in, inv,
                 gu_sem, wd_sem, wo_sem, wqkv_sem, x_sem, ho_sem, yo_sem, st_send, st_recv, send, recv, free, hfree):
    size, width = part.shape
    q_width = obuf.shape[1]
    group = q_width // HEAD_DIM
    gu_tiles = wg_ref.shape[1] // GU
    dn_tiles = width // DN
    per_slot = dn_tiles // 2
    per_chunk = gu_tiles + dn_tiles
    me = lax.axis_index('tp')
    core = lax.rem(me, 2)
    xi = lax.rem(lax.div(me, 2), 2)
    yi = lax.div(me, 4)
    partners = (me + 1 - 2 * core, me + 2 - 4 * xi, me + 4 - 8 * yi)
    core_dev = partners[0]
    parts = 4
    quarter = size // parts
    n0, n1, n2 = quarter // 2, quarter // 4, quarter // 8
    first, second = (xi, yi), (yi, xi)
    first_dev, second_dev = partners[1:], partners[:0:-1]

    barrier = pltpu.get_barrier_semaphore()
    for r in range(1, tp_size):
        pl.semaphore_signal(barrier, inc=1, device_id={'tp': lax.rem(me + r, tp_size)}, device_id_type=MESH)

    def rows(start, count):
        return pl.ds(pl.multiple_of(start, BLK), count)

    def remote(stream, phase, p, chunk):
        col = p % 2
        a = p * quarter + core * n0
        b = a + first[col] * n1
        own = b + second[col] * n2
        if phase == 0:
            src, dst, dev = part.at[rows(p * quarter + (1 - core) * n0, n0)], r0.at[stream, pl.ds(p * n0, n0)], core_dev
        elif phase == 1:
            src, dst, dev = r0.at[stream, rows(p * n0 + (1 - first[col]) * n1, n1)], r1.at[stream, pl.ds(p * n1, n1)], first_dev[col]
        elif phase == 2:
            src, dst, dev = r1.at[stream, rows(p * n1 + (1 - second[col]) * n2, n2)], r2.at[stream, pl.ds(p * n2, n2)], second_dev[col]
        else:
            start, count, dev = ((own, n2, second_dev[col]), (b, n1, first_dev[col]), (a, n0, core_dev))[phase - 3]
            if stream == 0:
                src = dst = h.at[lax.rem(chunk, 2), rows(start, count)]
            else:
                dst = y_ref.at[rows(chunk * size + start, count)]
                src = yo.at[pl.ds(p * n2, n2)] if phase == 3 else dst
        return pltpu.make_async_remote_copy(src_ref=src, dst_ref=dst, send_sem=send.at[stream, chunk, phase, p], recv_sem=recv.at[stream, chunk, phase, p], device_id={'tp': dev}, device_id_type=MESH)

    def own_row(p):
        return p * quarter + core * n0 + first[p % 2] * n1 + second[p % 2] * n2

    def base_copy(p, chunk):
        return pltpu.make_async_copy(x_ref.at[rows(chunk * size + own_row(p), n2)], ho.at[chunk, pl.ds(p * n2, n2)], ho_sem.at[chunk, p])

    def y_copy(p, chunk):
        return pltpu.make_async_copy(yo.at[pl.ds(p * n2, n2)], y_ref.at[rows(chunk * size + own_row(p), n2)], yo_sem.at[p])

    def x_copy(chunk):
        return pltpu.make_async_copy(x_ref.at[rows(chunk * size, size)], h.at[1], x_sem)

    def wo_copies():
        return [pltpu.make_async_copy(wo_ref.at[:, pl.ds(k * DN, DN)], wdb.at[k // per_slot, pl.ds(k % per_slot * q_width, q_width)], wo_sem.at[k]) for k in range(dn_tiles)]

    def qkv_copies():
        return (pltpu.make_async_copy(wq_ref, wgu.at[0, :, pl.ds(0, q_width)], wqkv_sem.at[0]),
                pltpu.make_async_copy(wk_ref, wgu.at[0, :, pl.ds(q_width, HEAD_DIM)], wqkv_sem.at[1]),
                pltpu.make_async_copy(wv_ref, wgu.at[1, :, pl.ds(0, HEAD_DIM)], wqkv_sem.at[2]))

    def gu_copies(chunk, j):
        slot = lax.rem(chunk * gu_tiles + j, 2)
        cols = pl.ds(pl.multiple_of(j * GU, GU), GU)
        return (pltpu.make_async_copy(wg_ref.at[:, cols], wgu.at[slot, :, pl.ds(0, GU)], gu_sem.at[slot, 0]),
                pltpu.make_async_copy(wu_ref.at[:, cols], wgu.at[slot, :, pl.ds(GU, GU)], gu_sem.at[slot, 1]))

    def dn_copy(k):
        slot = lax.rem(k, 2)
        return pltpu.make_async_copy(wd_ref.at[:, pl.ds(pl.multiple_of(k * DN, DN), DN)], wdb.at[slot], wd_sem.at[slot])

    def stat_copy(r, chunk):
        return pltpu.make_async_remote_copy(src_ref=stat.at[chunk], dst_ref=stat_in.at[chunk, r - 1], send_sem=st_send.at[chunk, r - 1], recv_sem=st_recv.at[chunk, r - 1], device_id={'tp': lax.rem(me + r, tp_size)}, device_id_type=MESH)

    def release_h():
        for i, dev in enumerate(partners):
            pl.semaphore_signal(hfree.at[i], inc=1, device_id={'tp': dev}, device_id_type=MESH)

    def add_into(dst, dst_start, src, src_start, count):
        @pl.loop(0, count // BLK)
        def _(i):
            d = pl.ds(pl.multiple_of(dst_start + i * BLK, BLK), BLK)
            s = pl.ds(pl.multiple_of(src_start + i * BLK, BLK), BLK)
            dst[d, :] = (dst[d, :].astype(jnp.float32) + src[s, :].astype(jnp.float32)).astype(jnp.bfloat16)

    def project_qkv(chunk):
        @pl.when(chunk == 0)
        def _():
            for cp in qkv_copies():
                cp.wait()
        x_copy(chunk).wait()
        qk[...] = jnp.dot(h[1], wgu[0], preferred_element_type=jnp.float32)
        vc_ref[rows(chunk * size, size), :] = jnp.dot(h[1], wgu[1, :, pl.ds(0, HEAD_DIM)], preferred_element_type=jnp.float32).astype(jnp.bfloat16)

        @pl.when(chunk + 1 < CHUNKS)
        def _():
            x_copy(chunk + 1).start()

        @pl.when(chunk + 1 == CHUNKS)
        def _():
            release_h()
            for cp in gu_copies(0, 0):
                cp.start()
        sums = []
        for blk in range(size // STAT):
            r = pl.ds(blk * STAT, STAT)
            squares = [jnp.square(qk[r, pl.ds(t * HEAD_DIM, HEAD_DIM)]) for t in range(group + 1)]
            for sq in (sum(squares[1:group], squares[0]), squares[group]):
                sums.append(jnp.sum(sq.T, axis=0, keepdims=True))
        stat[chunk] = jnp.concatenate(sums, axis=0)
        for r in range(1, tp_size):
            stat_copy(r, chunk).start()

    def attend(chunk):
        total = stat[chunk]
        for r in range(1, tp_size):
            stat_copy(r, chunk).wait()
        for r in range(1, tp_size):
            total = total + stat_in[chunk, r - 1]
        inv[0] = lax.rsqrt(total / (q_width * tp_size) + NORM_EPS)
        inv[1] = lax.rsqrt(total / (HEAD_DIM * tp_size) + NORM_EPS)
        cos, sin = cos_ref[...], sin_ref[...]
        gk = gk_ref[...].astype(jnp.float32)
        row = lax.broadcasted_iota(jnp.int32, (seq_len, seq_len), 0)
        col = lax.broadcasted_iota(jnp.int32, (seq_len, seq_len), 1)

        def rope(t):
            return t * cos + pltpu.roll(t, HEAD_DIM // 2, 1) * sin

        @pl.loop(0, size // STAT)
        def _(blk):
            iq = jnp.broadcast_to(inv[0, pl.ds(2 * blk, 1), :], (STAT, HEAD_DIM)).T
            ik = jnp.broadcast_to(inv[1, pl.ds(2 * blk + 1, 1), :], (STAT, HEAD_DIM)).T
            for b in range(STAT // seq_len):
                local = pl.ds(pl.multiple_of(blk * STAT + b * seq_len, seq_len), seq_len)
                mine = pl.ds(pl.multiple_of(chunk * size + blk * STAT + b * seq_len, seq_len), seq_len)
                inv_q, inv_k = iq[b * seq_len:(b + 1) * seq_len, :], ik[b * seq_len:(b + 1) * seq_len, :]
                keys = rope(qk[local, pl.ds(q_width, HEAD_DIM)] * inv_k * gk).astype(jnp.bfloat16)
                kc_ref[mine, :] = keys
                qs = []
                for hd in range(group):
                    cols = pl.ds(hd * HEAD_DIM, HEAD_DIM)
                    qs.append(rope(qk[local, cols] * inv_q * gq_ref[:, cols].astype(jnp.float32)).astype(jnp.bfloat16))
                queries = jnp.concatenate(qs, axis=0)
                scores = lax.dot_general(queries, keys, (((1,), (1,)), ((), ())), preferred_element_type=jnp.float32) * HEAD_DIM ** -0.5
                length = lens_ref[chunk * (size // seq_len) + blk * (STAT // seq_len) + b]
                allowed = ((col <= row) & (col < length)).astype(jnp.int32)
                scores = jnp.where(jnp.concatenate([allowed] * group, axis=0) > 0, scores, -1e30)
                e = jnp.exp(scores - jnp.max(scores, axis=-1, keepdims=True))
                probs = (e / jnp.sum(e, axis=-1, keepdims=True)).astype(jnp.bfloat16)
                out = jnp.dot(probs, vc_ref[mine, :], preferred_element_type=jnp.float32).astype(jnp.bfloat16)
                for hd in range(group):
                    obuf[mine, pl.ds(hd * HEAD_DIM, HEAD_DIM)] = out[hd * seq_len:(hd + 1) * seq_len, :]

    def project(chunk):
        @pl.when(chunk == 0)
        def _():
            for cp in wo_copies():
                cp.wait()

        @pl.loop(0, dn_tiles)
        def _(k):
            w = wdb[lax.div(k, per_slot), pl.ds(pl.multiple_of(lax.rem(k, per_slot) * q_width, q_width), q_width), :]
            cols = pl.ds(pl.multiple_of(k * DN, DN), DN)
            part[:, cols] = jnp.dot(obuf[rows(chunk * size, size), :], w, preferred_element_type=jnp.float32).astype(jnp.bfloat16)

    def take(sem, chunk):
        @pl.when(chunk >= 1)
        def _():
            pl.semaphore_wait(sem, 1)

    def give(sem, chunk, dev):
        @pl.when(chunk + 1 < CHUNKS)
        def _():
            pl.semaphore_signal(sem, inc=1, device_id={'tp': dev}, device_id_type=MESH)

    def event(stream, e, chunk):
        for p in range(parts):
            col = p % 2
            if e > 0:
                prev = remote(stream, e - 1, p, chunk)
                prev.wait_recv()
                prev.wait_send()
            if e == 1:
                add_into(r0.at[stream], p * n0, part, p * quarter + core * n0, n0)
            elif e == 2:
                add_into(r1.at[stream], p * n1, r0.at[stream], p * n0 + first[col] * n1, n1)
                give(free.at[stream, 0, p], chunk, core_dev)
            elif e == 3:
                gain = ga_ref if stream == 0 else gm_ref
                mine = pl.ds(p * n2, n2)
                kept = rows(p * n1 + second[col] * n2, n2)
                total = (r2[stream, mine, :].astype(jnp.float32) + r1[stream, kept, :].astype(jnp.float32)).astype(jnp.bfloat16)
                if stream == 0:
                    base_copy(p, chunk).wait()
                out = post_norm(ho[chunk, mine, :], total, gain[...])
                if stream == 0:
                    if p == 0:
                        for i in range(len(partners)):
                            take(hfree.at[i], chunk)
                    h[lax.rem(chunk, 2), rows(own_row(p), n2), :] = out
                    ho[chunk, mine, :] = out
                else:
                    yo[mine, :] = out
                    y_copy(p, chunk).start()
                give(free.at[stream, 1, p], chunk, first_dev[col])
                give(free.at[stream, 2, p], chunk, second_dev[col])
            elif e == 4 and stream == 1:
                y_copy(p, chunk).wait()
            if e < 3:
                take(free.at[stream, e, p], chunk)
            if e < 6:
                remote(stream, e, p, chunk).start()

    for cp in qkv_copies():
        cp.start()
    x_copy(0).start()
    for cp in wo_copies():
        cp.start()
    for chunk in range(CHUNKS):
        for p in range(parts):
            base_copy(p, chunk).start()
    pl.semaphore_wait(barrier, tp_size - 1)

    reload_wo = sorted({(s - PROLOGUE) // per_chunk for s in EVENTS[0, 0] if s >= PROLOGUE} - {0})

    @pl.loop(0, STEPS)
    def _(g):
        gm = g - PROLOGUE
        c, j = lax.div(gm, per_chunk), lax.rem(gm, per_chunk)
        computes = (gm >= 0) & (gm < CHUNKS * per_chunk)

        for it in reload_wo:
            @pl.when(gm == it * per_chunk + 1)
            def _():
                for cp in wo_copies():
                    cp.wait()

        for (stream, e), at in EVENTS.items():
            hit = functools.reduce(lambda a, b: a | b, [g == s for s in at])

            @pl.when(hit)
            def _():
                chunk = sum([(g >= s).astype(jnp.int32) for s in at[1:]])
                if stream == 2:
                    (project_qkv, attend)[e](chunk)
                else:
                    if (stream, e) == (0, 0):
                        project(chunk)
                    event(stream, e, chunk)

        @pl.when(computes & (j < gu_tiles))
        def _():
            for cp in gu_copies(c, j):
                cp.wait()

            @pl.when((j + 1 < gu_tiles) | (c + 1 < CHUNKS))
            def _():
                wraps = (j + 1 >= gu_tiles).astype(jnp.int32)
                for cp in gu_copies(c + wraps, (j + 1) * (1 - wraps)):
                    cp.start()

            @pl.when(j == gu_tiles - 2)
            def _():
                dn_copy(0).start()
            slot = lax.rem(c * gu_tiles + j, 2)
            both = jnp.dot(h[lax.rem(c, 2)], wgu[slot], preferred_element_type=jnp.float32)
            gate, up = both[:, :GU], both[:, GU:]
            act[:, pl.ds(pl.multiple_of(j * GU, GU), GU)] = (gate * lax.logistic(gate) * up).astype(jnp.bfloat16)

            @pl.when((j == gu_tiles - 1) & (c + 2 < CHUNKS))
            def _():
                release_h()

        @pl.when(computes & (j >= gu_tiles))
        def _():
            k = j - gu_tiles
            dn_copy(k).wait()

            @pl.when(k + 1 < dn_tiles)
            def _():
                dn_copy(k + 1).start()
            part[:, pl.ds(pl.multiple_of(k * DN, DN), DN)] = jnp.dot(act[...], wdb[lax.rem(k, 2)], preferred_element_type=jnp.float32).astype(jnp.bfloat16)

            @pl.when(k + 1 == dn_tiles)
            def _():
                event(1, 0, c)
            for it in reload_wo:
                @pl.when(gm == it * per_chunk - 1)
                def _():
                    for cp in wo_copies():
                        cp.start()


def solution(mesh):
    tp_size = mesh.shape['tp']

    def local_layer(tokens, seq_lens, w_q, w_k, w_v, w_o, g_q, g_k, g_attn, g_mlp, w_gate, w_up, w_down):
        prompts, seq_len, width = tokens.shape
        total, inner, q_width = prompts * seq_len, w_gate.shape[1], w_q.shape[1]
        size = total // CHUNKS
        cos, sin = rope_tables(seq_len, HEAD_DIM)
        bf, f32 = jnp.bfloat16, jnp.float32
        anyspec = pl.BlockSpec(memory_space=pl.ANY)
        vmem = pl.BlockSpec(memory_space=pltpu.VMEM)
        dma, credit = pltpu.SemaphoreType.DMA, pltpu.SemaphoreType.REGULAR
        kv = jax.ShapeDtypeStruct((total, HEAD_DIM), bf)
        y, keys, v = pl.pallas_call(
            functools.partial(layer_kernel, seq_len, tp_size),
            out_shape=[jax.ShapeDtypeStruct((total, width), bf), kv, kv],
            in_specs=[pl.BlockSpec(memory_space=pltpu.SMEM)] + [anyspec] * 8 + [vmem] * 6,
            out_specs=[anyspec, vmem, vmem],
            scratch_shapes=[
                pltpu.VMEM((2, width, 2 * GU), bf), pltpu.VMEM((2, inner, DN), bf), pltpu.VMEM((2, size, width), bf),
                pltpu.VMEM((size, inner), bf), pltpu.VMEM((size, width), bf),
                pltpu.VMEM((2, size // 2, width), bf), pltpu.VMEM((2, size // 4, width), bf), pltpu.VMEM((2, size // 8, width), bf),
                pltpu.VMEM((total, q_width), bf), pltpu.VMEM((size, q_width + HEAD_DIM), f32),
                pltpu.VMEM((CHUNKS, size // 8, width), bf), pltpu.VMEM((size // 8, width), bf),
                pltpu.VMEM((CHUNKS, 8, STAT), f32), pltpu.VMEM((CHUNKS, tp_size - 1, 8, STAT), f32), pltpu.VMEM((2, 8, STAT), f32),
                dma((2, 2)), dma((2,)), dma((width // DN,)), dma((3,)), dma, dma((CHUNKS, 4)), dma((4,)),
                dma((CHUNKS, tp_size - 1)), dma((CHUNKS, tp_size - 1)), dma((2, CHUNKS, 6, 4)), dma((2, CHUNKS, 6, 4)),
                credit((2, 3, 4)), credit((3,)),
            ],
            compiler_params=pltpu.CompilerParams(collective_id=0, has_side_effects=True, vmem_limit_bytes=67043328),
            cost_estimate=pl.CostEstimate(flops=2 * total * width * (3 * inner + 2 * q_width + 2 * HEAD_DIM), bytes_accessed=CHUNKS * 3 * inner * width * 2, transcendentals=total * inner),
        )(seq_lens, tokens.reshape(total, width), w_q, w_k, w_v, w_o, w_gate, w_up, w_down,
          g_q[None], g_k[None], g_attn[None], g_mlp[None], jnp.asarray(cos), jnp.asarray(sin))
        cache = (prompts, 1, seq_len, HEAD_DIM)
        return y.reshape(prompts, seq_len, width), keys.reshape(cache), v.reshape(cache)

    return jax.shard_map(local_layer, mesh=mesh, in_specs=(P('dp', None, None), P('dp'), P(None, 'tp'), P(None, 'tp'), P(None, 'tp'), P('tp', None), P('tp'), P('tp'), P(), P(), P(None, 'tp'), P(None, 'tp'), P('tp', None)), out_specs=(P('dp', None, None), P('dp', 'tp', None, None), P('dp', 'tp', None, None)), check_vma=False)
```

time: 1000 us -> 464 us (0.46)
  waiting for transfers between devices: 502 us -> 0 us
  Pallas kernels: 0 us -> 440 us
  matrix products: 335 us -> 0 us
  other arithmetic: 85 us -> 0 us
  blocking collectives: 25.5 us -> 0 us
  between operations: 14.7 us -> 0.66 us
  local copies, waits for them, and re-layouts: 35.1 us -> 23.1 us
    psum x2 -> x0, waiting for transfers between devices: 502 us -> none  [the longest x1 252 us: local_layer(): attn_proj = lax.psum(attn_part, 'tp')]
    pallas_call x0 -> x1, Pallas kernels: none -> 440 us  [local_layer(): pl.pallas_call(functools.partial(layer_kernel, seq_len, tp_size), out_sha...]
    dot_general x9 -> x0, matrix products: 335 us -> none  [the longest x1 94 us: local_layer(): jnp.einsum('bsd,df->bsf', hidden, w_gate, preferred_element_type=jnp.floa...]
    convert_element_type x8 -> x0, other arithmetic: 46.8 us -> none  [the longest x2 40.7 us: post_norm(): (base.astype(jnp.float32) + branch32 * rms_scale(branch32) * gain.astype(...]
    psum x1 -> x0, blocking collectives: 25.5 us -> none  [local_layer(): q_sumsq = lax.psum(jnp.sum(q_raw * q_raw, axis=-1, keepdims=True), 'tp')]
    reshape x3 -> x0, local copies, waits for them, and re-layouts: 21.8 us -> none  [the longest x2 14.7 us: local_layer(): q_norm.reshape(prompts, seq_len, kv_local, group_size, HEAD_DIM)]
    reduce_sum x3 -> x0, other arithmetic: 20.6 us -> none  [the longest x2 18.7 us: rms_scale(): return lax.rsqrt(jnp.mean(vals * vals, axis=-1, keepdims=True) + NORM_EPS)]
    concatenate x2 -> x0, other arithmetic: 11.2 us -> none  [apply_rope(): jnp.concatenate([-vecs[..., half_dim:], vecs[..., :half_dim]], axis=-1)]
  transfers between devices with their start and end apart: 2 -> 0, of which waited for: 2 -> 0; matrix products, arithmetic and copies ran while one was open for 0% -> 0% of each run, Pallas kernels for 0% -> 0%
where the time goes in v3:
time: 464 us
  Pallas kernels  440 us (95%)
  local copies, waits for them, and re-layouts  23.1 us (5%)
    pallas_call x1, Pallas kernels, local_layer(): pl.pallas_call(functools.partial(layer_kernel, seq_len, tp_size), out_sha...  440 us
    unnamed x7, local copies, waits for them, and re-layouts  19.2 us

profile of v3, /device:TPU:0, one launch (start us, length us, event | category | flops | bytes accessed | tf_op | source)
XLA Modules:
  0.0 463.8 jit_solution(13258380578938501234)
XLA Ops:
  0.6 1.3 broadcast_in_dim.12.gq_ref
  1.9 1.3 broadcast_in_dim.14.ga_ref
  3.2 1.3 broadcast_in_dim.15.gm_ref
  4.5 440.1 %shard_map.166 = (bf16[2048,5120]{1,0:T(8,128)(2,1)}, bf16[2048,128]{1,0:T(8,128)(2,1)}, bf16[2048,128]{1,0:T(8,128)(2,1)}) custom-call(s32[32]{0:T(128)} %lens_ref.1, bf16[2048,5120]{1,0:T(8,128)(2,1)} %bitcast.12, bf16[5120,640]{1,0:T(8,128)(2,1)} %wq_ref.1, bf16[5120,128]{1,0:T(8,128)(2,1)} %wk_ref.1, bf16[5120,128]{1,0:T(8,128)(2,1)} %wv_ref.1, ...), custom_call_target="tpu_custom_call" | custom-call | flops 249644974080 | bytes 424673280 | tf_op jit(solution)/shard_map/pallas_call | solution.py:374
  444.6 0.0 copy-start.1
  444.6 0.0 copy-start
  444.6 17.6 %copy.23 = bf16[32,64,5120]{2,1,0:T(8,128)(2,1)} copy(bf16[32,64,5120]{2,1,0:T(8,128)(2,1)} %bitcast.9) | data formatting | bytes 41943040
  462.2 0.0 copy-done.1
  462.2 0.8 copy.24
  463.0 0.0 copy-done
  463.0 0.8 copy.25
Async XLA Ops:
  444.6 17.7 %copy-start.1 = (bf16[2048,128]{1,0:T(8,128)(2,1)S(1)}, bf16[2048,128]{1,0:T(8,128)(2,1)}, u32[]{:S(2)}) copy-start(bf16[2048,128]{1,0:T(8,128)(2,1)} %get-tuple-element.7) | copy-start | bytes 1572868
  444.6 18.4 %copy-start = (bf16[2048,128]{1,0:T(8,128)(2,1)S(1)}, bf16[2048,128]{1,0:T(8,128)(2,1)}, u32[]{:S(2)}) copy-start(bf16[2048,128]{1,0:T(8,128)(2,1)} %get-tuple-element.8) | copy-start | bytes 1572868

commit v4 on v3

--- a/solution.py
+++ b/solution.py
@@ -18,23 +18,23 @@
 BLK = 16
 STAT = 128
 
-PROLOGUE, STEPS = 19, 103
+PROLOGUE, STEPS = 22, 107
 EVENTS = {
-    (2, 0): (0, 3, 6, 13),
-    (2, 1): (1, 5, 11, 16),
-    (0, 6): (18, 29, 43, 60),
-    (0, 5): (17, 27, 41, 59),
-    (0, 4): (12, 22, 32, 51),
-    (0, 3): (9, 20, 28, 47),
-    (0, 2): (7, 14, 25, 38),
-    (0, 1): (4, 10, 20, 28),
-    (0, 0): (2, 8, 15, 25),
-    (1, 6): (64, 79, 97, 102),
-    (1, 5): (62, 78, 95, 101),
-    (1, 4): (54, 71, 87, 100),
-    (1, 3): (47, 66, 84, 99),
-    (1, 2): (45, 64, 82, 98),
-    (1, 1): (39, 59, 78, 96),
+    (2, 0): (2, 7, 18, 21),
+    (2, 1): (2, 12, 20, 23),
+    (0, 6): (22, 40, 60, 76),
+    (0, 5): (20, 36, 53, 71),
+    (0, 4): (15, 29, 43, 65),
+    (0, 3): (12, 24, 31, 56),
+    (0, 2): (7, 23, 28, 45),
+    (0, 1): (4, 18, 25, 31),
+    (0, 0): (2, 13, 23, 28),
+    (1, 6): (99, 101, 103, 106),
+    (1, 5): (98, 99, 101, 105),
+    (1, 4): (69, 85, 93, 104),
+    (1, 3): (61, 79, 88, 101),
+    (1, 2): (53, 73, 84, 100),
+    (1, 1): (44, 62, 80, 98),
 }
 
 
@@ -128,12 +128,18 @@
     def gu_copies(chunk, j):
         slot = lax.rem(chunk * gu_tiles + j, 2)
         cols = pl.ds(pl.multiple_of(j * GU, GU), GU)
-        return (pltpu.make_async_copy(wg_ref.at[:, cols], wgu.at[slot, :, pl.ds(0, GU)], gu_sem.at[slot, 0]),
-                pltpu.make_async_copy(wu_ref.at[:, cols], wgu.at[slot, :, pl.ds(GU, GU)], gu_sem.at[slot, 1]))
-
-    def dn_copy(k):
-        slot = lax.rem(k, 2)
-        return pltpu.make_async_copy(wd_ref.at[:, pl.ds(pl.multiple_of(k * DN, DN), DN)], wdb.at[slot], wd_sem.at[slot])
+        depth = width // 2
+        return [pltpu.make_async_copy(w.at[pl.ds(b * depth, depth), cols], wgu.at[slot, pl.ds(b * depth, depth), pl.ds(a * GU, GU)], gu_sem.at[slot, a, b])
+                for a, w in enumerate((wg_ref, wu_ref)) for b in range(2)]
+
+    def dn_copies(k):
+        slot, depth = lax.rem(k, 2), wd_ref.shape[0] // 2
+        cols = pl.ds(pl.multiple_of(k * DN, DN), DN)
+        return [pltpu.make_async_copy(wd_ref.at[pl.ds(b * depth, depth), cols], wdb.at[slot, pl.ds(b * depth, depth)], wd_sem.at[slot, b]) for b in range(2)]
+
+    def launch(copies):
+        for cp in copies:
+            cp.start()
 
     def stat_copy(r, chunk):
         return pltpu.make_async_remote_copy(src_ref=stat.at[chunk], dst_ref=stat_in.at[chunk, r - 1], send_sem=st_send.at[chunk, r - 1], recv_sem=st_recv.at[chunk, r - 1], device_id={'tp': lax.rem(me + r, tp_size)}, device_id_type=MESH)
@@ -165,8 +171,7 @@
         @pl.when(chunk + 1 == CHUNKS)
         def _():
             release_h()
-            for cp in gu_copies(0, 0):
-                cp.start()
+            launch(gu_copies(0, 0))
         sums = []
         for blk in range(size // STAT):
             r = pl.ds(blk * STAT, STAT)
@@ -186,7 +191,7 @@
         inv[0] = lax.rsqrt(total / (q_width * tp_size) + NORM_EPS)
         inv[1] = lax.rsqrt(total / (HEAD_DIM * tp_size) + NORM_EPS)
         cos, sin = cos_ref[...], sin_ref[...]
-        gk = gk_ref[...].astype(jnp.float32)
+        gk = gk_ref[...].astype(jnp.float32)[None, :]
         row = lax.broadcasted_iota(jnp.int32, (seq_len, seq_len), 0)
         col = lax.broadcasted_iota(jnp.int32, (seq_len, seq_len), 1)
 
@@ -206,7 +211,7 @@
                 qs = []
                 for hd in range(group):
                     cols = pl.ds(hd * HEAD_DIM, HEAD_DIM)
-                    qs.append(rope(qk[local, cols] * inv_q * gq_ref[:, cols].astype(jnp.float32)).astype(jnp.bfloat16))
+                    qs.append(rope(qk[local, cols] * inv_q * gq_ref[cols].astype(jnp.float32)[None, :]).astype(jnp.bfloat16))
                 queries = jnp.concatenate(qs, axis=0)
                 scores = lax.dot_general(queries, keys, (((1,), (1,)), ((), ())), preferred_element_type=jnp.float32) * HEAD_DIM ** -0.5
                 length = lens_ref[chunk * (size // seq_len) + blk * (STAT // seq_len) + b]
@@ -259,7 +264,7 @@
                 total = (r2[stream, mine, :].astype(jnp.float32) + r1[stream, kept, :].astype(jnp.float32)).astype(jnp.bfloat16)
                 if stream == 0:
                     base_copy(p, chunk).wait()
-                out = post_norm(ho[chunk, mine, :], total, gain[...])
+                out = post_norm(ho[chunk, mine, :], total, gain[...][None, :])
                 if stream == 0:
                     if p == 0:
                         for i in range(len(partners)):
@@ -323,12 +328,11 @@
             @pl.when((j + 1 < gu_tiles) | (c + 1 < CHUNKS))
             def _():
                 wraps = (j + 1 >= gu_tiles).astype(jnp.int32)
-                for cp in gu_copies(c + wraps, (j + 1) * (1 - wraps)):
-                    cp.start()
+                launch(gu_copies(c + wraps, (j + 1) * (1 - wraps)))
 
             @pl.when(j == gu_tiles - 2)
             def _():
-                dn_copy(0).start()
+                launch(dn_copies(0))
             slot = lax.rem(c * gu_tiles + j, 2)
             both = jnp.dot(h[lax.rem(c, 2)], wgu[slot], preferred_element_type=jnp.float32)
             gate, up = both[:, :GU], both[:, GU:]
@@ -341,11 +345,12 @@
         @pl.when(computes & (j >= gu_tiles))
         def _():
             k = j - gu_tiles
-            dn_copy(k).wait()
+            for cp in dn_copies(k):
+                cp.wait()
 
             @pl.when(k + 1 < dn_tiles)
             def _():
-                dn_copy(k + 1).start()
+                launch(dn_copies(k + 1))
             part[:, pl.ds(pl.multiple_of(k * DN, DN), DN)] = jnp.dot(act[...], wdb[lax.rem(k, 2)], preferred_element_type=jnp.float32).astype(jnp.bfloat16)
 
             @pl.when(k + 1 == dn_tiles)
@@ -356,6 +361,37 @@
                 def _():
                     for cp in wo_copies():
                         cp.start()
+
+
+def store_kernel(y_ref, k_ref, v_ref, y_out, k_out, v_out, buf, kv, get, put):
+    pieces, rows = buf.shape[0], buf.shape[1]
+    def piece(i):
+        return pl.ds(i * rows, rows)
+    loads = [pltpu.make_async_copy(src, kv.at[i], get.at[pieces + i]) for i, src in enumerate((k_ref, v_ref))]
+    loads += [pltpu.make_async_copy(y_ref.at[piece(i)], buf.at[i], get.at[i]) for i in range(pieces)]
+    stores = [pltpu.make_async_copy(kv.at[i], dst, put.at[pieces + i]) for i, dst in enumerate((k_out, v_out))]
+    stores += [pltpu.make_async_copy(buf.at[i], y_out.at[piece(i)], put.at[i]) for i in range(pieces)]
+    for cp in loads:
+        cp.start()
+    for load, store in zip(loads, stores):
+        load.wait()
+        store.start()
+    for cp in stores:
+        cp.wait()
+
+
+def store(y, keys, v):
+    pieces = 16
+    anyspec = pl.BlockSpec(memory_space=pl.ANY)
+    dma = pltpu.SemaphoreType.DMA
+    return pl.pallas_call(
+        store_kernel,
+        out_shape=[jax.ShapeDtypeStruct(t.shape, t.dtype) for t in (y, keys, v)],
+        in_specs=[anyspec] * 3,
+        out_specs=[anyspec] * 3,
+        scratch_shapes=[pltpu.VMEM((pieces, y.shape[0] // pieces, y.shape[1]), y.dtype), pltpu.VMEM((2,) + keys.shape, keys.dtype), dma((pieces + 2,)), dma((pieces + 2,))],
+        compiler_params=pltpu.CompilerParams(vmem_limit_bytes=67043328),
+    )(y, keys, v)
 
 
 def solution(mesh):
@@ -383,14 +419,15 @@
                 pltpu.VMEM((total, q_width), bf), pltpu.VMEM((size, q_width + HEAD_DIM), f32),
                 pltpu.VMEM((CHUNKS, size // 8, width), bf), pltpu.VMEM((size // 8, width), bf),
                 pltpu.VMEM((CHUNKS, 8, STAT), f32), pltpu.VMEM((CHUNKS, tp_size - 1, 8, STAT), f32), pltpu.VMEM((2, 8, STAT), f32),
-                dma((2, 2)), dma((2,)), dma((width // DN,)), dma((3,)), dma, dma((CHUNKS, 4)), dma((4,)),
+                dma((2, 2, 2)), dma((2, 2)), dma((width // DN,)), dma((3,)), dma, dma((CHUNKS, 4)), dma((4,)),
                 dma((CHUNKS, tp_size - 1)), dma((CHUNKS, tp_size - 1)), dma((2, CHUNKS, 6, 4)), dma((2, CHUNKS, 6, 4)),
                 credit((2, 3, 4)), credit((3,)),
             ],
             compiler_params=pltpu.CompilerParams(collective_id=0, has_side_effects=True, vmem_limit_bytes=67043328),
             cost_estimate=pl.CostEstimate(flops=2 * total * width * (3 * inner + 2 * q_width + 2 * HEAD_DIM), bytes_accessed=CHUNKS * 3 * inner * width * 2, transcendentals=total * inner),
         )(seq_lens, tokens.reshape(total, width), w_q, w_k, w_v, w_o, w_gate, w_up, w_down,
-          g_q[None], g_k[None], g_attn[None], g_mlp[None], jnp.asarray(cos), jnp.asarray(sin))
+          g_q, g_k, g_attn, g_mlp, jnp.asarray(cos), jnp.asarray(sin))
+        y, keys, v = store(y, keys, v)
         cache = (prompts, 1, seq_len, HEAD_DIM)
         return y.reshape(prompts, seq_len, width), keys.reshape(cache), v.reshape(cache)
 

time: 464 us -> 456 us (0.983)
  local copies, waits for them, and re-layouts: 23.1 us -> 0 us
  Pallas kernels: 440 us -> 455 us
    unnamed x7 -> x0, local copies, waits for them, and re-layouts: 19.2 us -> none
    pallas_call x0 -> x1, Pallas kernels: none -> 15.4 us  [store(): pl.pallas_call(store_kernel, out_shape=[jax.ShapeDtypeStruct(t.shape, t.d...]
where the time goes in v4:
time: 456 us; the launch traced here: 455 us
  Pallas kernels  455 us (100%)
    pallas_call x1, Pallas kernels, local_layer(): pl.pallas_call(functools.partial(layer_kernel, seq_len, tp_size), out_sha...  439 us
    pallas_call x1, Pallas kernels, store(): pl.pallas_call(store_kernel, out_shape=[jax.ShapeDtypeStruct(t.shape, t.d...  15.4 us

profile of v4, /device:TPU:0, one launch (start us, length us, event | category | flops | bytes accessed | tf_op | source)
XLA Modules:
  0.0 455.3 jit_solution(3593140675483736354)
XLA Ops:
  0.6 439.3 %shard_map.166 = (bf16[2048,5120]{1,0:T(8,128)(2,1)}, bf16[2048,128]{1,0:T(8,128)(2,1)}, bf16[2048,128]{1,0:T(8,128)(2,1)}) custom-call(s32[32]{0:T(128)} %lens_ref.1, bf16[2048,5120]{1,0:T(8,128)(2,1)} %bitcast.8, bf16[5120,640]{1,0:T(8,128)(2,1)} %wq_ref.1, bf16[5120,128]{1,0:T(8,128)(2,1)} %wk_ref.1, bf16[5120,128]{1,0:T(8,128)(2,1)} %wv_ref.1, ...), custom_call_target="tpu_custom_call" | custom-call | flops 249644974080 | bytes 424673280 | tf_op jit(solution)/shard_map/pallas_call | solution.py:410
  440.0 15.4 %shard_map.167 = (bf16[2048,5120]{1,0:T(8,128)(2,1)}, bf16[2048,128]{1,0:T(8,128)(2,1)}, bf16[2048,128]{1,0:T(8,128)(2,1)}) custom-call(bf16[2048,5120]{1,0:T(8,128)(2,1)} %get-tuple-element.9.y_ref, bf16[2048,128]{1,0:T(8,128)(2,1)} %get-tuple-element.10.k_ref, bf16[2048,128]{1,0:T(8,128)(2,1)} %get-tuple-element.11.v_ref), custom_call_target="tpu_custom_call" | custom-call | tf_op jit(solution)/shard_map/pallas_call | solution.py:387

commit v5 on v4

--- a/solution.py
+++ b/solution.py
@@ -14,27 +14,27 @@
 MESH = pl.DeviceIdType.MESH
 CHUNKS = 4
 GU = 384
-DN = 512
+DN = 1024
 BLK = 16
 STAT = 128
 
-PROLOGUE, STEPS = 22, 107
+PROLOGUE, STEPS = 22, 87
 EVENTS = {
-    (2, 0): (2, 7, 18, 21),
-    (2, 1): (2, 12, 20, 23),
-    (0, 6): (22, 40, 60, 76),
-    (0, 5): (20, 36, 53, 71),
-    (0, 4): (15, 29, 43, 65),
-    (0, 3): (12, 24, 31, 56),
-    (0, 2): (7, 23, 28, 45),
-    (0, 1): (4, 18, 25, 31),
-    (0, 0): (2, 13, 23, 28),
-    (1, 6): (99, 101, 103, 106),
-    (1, 5): (98, 99, 101, 105),
-    (1, 4): (69, 85, 93, 104),
-    (1, 3): (61, 79, 88, 101),
-    (1, 2): (53, 73, 84, 100),
-    (1, 1): (44, 62, 80, 98),
+    (2, 0): (0, 3, 10, 19),
+    (2, 1): (1, 5, 12, 27),
+    (0, 6): (22, 36, 48, 64),
+    (0, 5): (18, 33, 46, 57),
+    (0, 4): (8, 29, 35, 50),
+    (0, 3): (5, 24, 31, 45),
+    (0, 2): (4, 23, 28, 41),
+    (0, 1): (2, 11, 25, 31),
+    (0, 0): (1, 6, 23, 28),
+    (1, 6): (81, 84, 85, 86),
+    (1, 5): (78, 80, 83, 84),
+    (1, 4): (52, 67, 75, 83),
+    (1, 3): (49, 64, 73, 81),
+    (1, 2): (46, 58, 71, 80),
+    (1, 1): (37, 51, 65, 78),
 }
 
 
@@ -57,14 +57,14 @@
 
 def layer_kernel(seq_len, tp_size, lens_ref, x_ref, wq_ref, wk_ref, wv_ref, wo_ref, wg_ref, wu_ref, wd_ref,
                  gq_ref, gk_ref, ga_ref, gm_ref, cos_ref, sin_ref, y_ref, kc_ref, vc_ref,
-                 wgu, wdb, h, act, part, r0, r1, r2, obuf, qk, ho, yo, stat, stat_in, inv,
-                 gu_sem, wd_sem, wo_sem, wqkv_sem, x_sem, ho_sem, yo_sem, st_send, st_recv, send, recv, free, hfree):
+                 wgu, wdb, h, act, part, r0, r1, r2, obuf, qk, kv, ho, stat, stat_in, inv,
+                 gu_sem, wd_sem, wo_sem, wqkv_sem, x_sem, kv_sem, ho_sem, yo_sem, st_send, st_recv, send, recv, free, hfree):
     size, width = part.shape
+    half = width // 2
     q_width = obuf.shape[1]
     group = q_width // HEAD_DIM
     gu_tiles = wg_ref.shape[1] // GU
     dn_tiles = width // DN
-    per_slot = dn_tiles // 2
     per_chunk = gu_tiles + dn_tiles
     me = lax.axis_index('tp')
     core = lax.rem(me, 2)
@@ -99,10 +99,10 @@
         else:
             start, count, dev = ((own, n2, second_dev[col]), (b, n1, first_dev[col]), (a, n0, core_dev))[phase - 3]
             if stream == 0:
-                src = dst = h.at[lax.rem(chunk, 2), rows(start, count)]
+                src = dst = h.at[lax.rem(chunk, 2), :, rows(start, count)]
             else:
                 dst = y_ref.at[rows(chunk * size + start, count)]
-                src = yo.at[pl.ds(p * n2, n2)] if phase == 3 else dst
+                src = ho.at[chunk, pl.ds(p * n2, n2)] if phase == 3 else dst
         return pltpu.make_async_remote_copy(src_ref=src, dst_ref=dst, send_sem=send.at[stream, chunk, phase, p], recv_sem=recv.at[stream, chunk, phase, p], device_id={'tp': dev}, device_id_type=MESH)
 
     def own_row(p):
@@ -112,13 +112,16 @@
         return pltpu.make_async_copy(x_ref.at[rows(chunk * size + own_row(p), n2)], ho.at[chunk, pl.ds(p * n2, n2)], ho_sem.at[chunk, p])
 
     def y_copy(p, chunk):
-        return pltpu.make_async_copy(yo.at[pl.ds(p * n2, n2)], y_ref.at[rows(chunk * size + own_row(p), n2)], yo_sem.at[p])
+        return pltpu.make_async_copy(ho.at[chunk, pl.ds(p * n2, n2)], y_ref.at[rows(chunk * size + own_row(p), n2)], yo_sem.at[p])
 
     def x_copy(chunk):
-        return pltpu.make_async_copy(x_ref.at[rows(chunk * size, size)], h.at[1], x_sem)
+        return [pltpu.make_async_copy(x_ref.at[rows(chunk * size, size), pl.ds(i * half, half)], h.at[1, i], x_sem.at[i]) for i in range(2)]
+
+    def times_h(par, w):
+        return sum(jnp.dot(h[par, i], w[i], preferred_element_type=jnp.float32) for i in range(2))
 
     def wo_copies():
-        return [pltpu.make_async_copy(wo_ref.at[:, pl.ds(k * DN, DN)], wdb.at[k // per_slot, pl.ds(k % per_slot * q_width, q_width)], wo_sem.at[k]) for k in range(dn_tiles)]
+        return [pltpu.make_async_copy(wo_ref.at[:, dn_cols(k, b)], wdb.at[1, b, pl.ds(k * q_width, q_width)], wo_sem.at[k, b]) for k in range(dn_tiles) for b in range(2)]
 
     def qkv_copies():
         return (pltpu.make_async_copy(wq_ref, wgu.at[0, :, pl.ds(0, q_width)], wqkv_sem.at[0]),
@@ -132,10 +135,15 @@
         return [pltpu.make_async_copy(w.at[pl.ds(b * depth, depth), cols], wgu.at[slot, pl.ds(b * depth, depth), pl.ds(a * GU, GU)], gu_sem.at[slot, a, b])
                 for a, w in enumerate((wg_ref, wu_ref)) for b in range(2)]
 
+    def dn_cols(k, b):
+        return pl.ds(pl.multiple_of(k * DN + b * (DN // 2), DN // 2), DN // 2)
+
     def dn_copies(k):
-        slot, depth = lax.rem(k, 2), wd_ref.shape[0] // 2
-        cols = pl.ds(pl.multiple_of(k * DN, DN), DN)
-        return [pltpu.make_async_copy(wd_ref.at[pl.ds(b * depth, depth), cols], wdb.at[slot, pl.ds(b * depth, depth)], wd_sem.at[slot, b]) for b in range(2)]
+        slot = lax.rem(k, 2)
+        return [pltpu.make_async_copy(wd_ref.at[:, dn_cols(k, b)], wdb.at[slot, b], wd_sem.at[slot, b]) for b in range(2)]
+
+    def kv_copies(chunk):
+        return [pltpu.make_async_copy(kv.at[i], out.at[rows(chunk * size, size)], kv_sem.at[i]) for i, out in enumerate((kc_ref, vc_ref))]
 
     def launch(copies):
         for cp in copies:
@@ -160,13 +168,19 @@
         def _():
             for cp in qkv_copies():
                 cp.wait()
-        x_copy(chunk).wait()
-        qk[...] = jnp.dot(h[1], wgu[0], preferred_element_type=jnp.float32)
-        vc_ref[rows(chunk * size, size), :] = jnp.dot(h[1], wgu[1, :, pl.ds(0, HEAD_DIM)], preferred_element_type=jnp.float32).astype(jnp.bfloat16)
+        for cp in x_copy(chunk):
+            cp.wait()
+        qk[...] = times_h(1, [wgu[0, pl.ds(i * half, half)] for i in range(2)])
+        @pl.when(chunk > 0)
+        def _():
+            for cp in kv_copies(chunk - 1):
+                cp.wait()
+        kv[1] = times_h(1, [wgu[1, pl.ds(i * half, half), pl.ds(0, HEAD_DIM)] for i in range(2)]).astype(jnp.bfloat16)
 
         @pl.when(chunk + 1 < CHUNKS)
         def _():
-            x_copy(chunk + 1).start()
+            for cp in x_copy(chunk + 1):
+                cp.start()
 
         @pl.when(chunk + 1 == CHUNKS)
         def _():
@@ -204,10 +218,9 @@
             ik = jnp.broadcast_to(inv[1, pl.ds(2 * blk + 1, 1), :], (STAT, HEAD_DIM)).T
             for b in range(STAT // seq_len):
                 local = pl.ds(pl.multiple_of(blk * STAT + b * seq_len, seq_len), seq_len)
-                mine = pl.ds(pl.multiple_of(chunk * size + blk * STAT + b * seq_len, seq_len), seq_len)
                 inv_q, inv_k = iq[b * seq_len:(b + 1) * seq_len, :], ik[b * seq_len:(b + 1) * seq_len, :]
                 keys = rope(qk[local, pl.ds(q_width, HEAD_DIM)] * inv_k * gk).astype(jnp.bfloat16)
-                kc_ref[mine, :] = keys
+                kv[0, local, :] = keys
                 qs = []
                 for hd in range(group):
                     cols = pl.ds(hd * HEAD_DIM, HEAD_DIM)
@@ -219,9 +232,10 @@
                 scores = jnp.where(jnp.concatenate([allowed] * group, axis=0) > 0, scores, -1e30)
                 e = jnp.exp(scores - jnp.max(scores, axis=-1, keepdims=True))
                 probs = (e / jnp.sum(e, axis=-1, keepdims=True)).astype(jnp.bfloat16)
-                out = jnp.dot(probs, vc_ref[mine, :], preferred_element_type=jnp.float32).astype(jnp.bfloat16)
+                out = jnp.dot(probs, kv[1, local, :], preferred_element_type=jnp.float32).astype(jnp.bfloat16)
                 for hd in range(group):
-                    obuf[mine, pl.ds(hd * HEAD_DIM, HEAD_DIM)] = out[hd * seq_len:(hd + 1) * seq_len, :]
+                    obuf[local, pl.ds(hd * HEAD_DIM, HEAD_DIM)] = out[hd * seq_len:(hd + 1) * seq_len, :]
+        launch(kv_copies(chunk))
 
     def project(chunk):
         @pl.when(chunk == 0)
@@ -231,9 +245,9 @@
 
         @pl.loop(0, dn_tiles)
         def _(k):
-            w = wdb[lax.div(k, per_slot), pl.ds(pl.multiple_of(lax.rem(k, per_slot) * q_width, q_width), q_width), :]
-            cols = pl.ds(pl.multiple_of(k * DN, DN), DN)
-            part[:, cols] = jnp.dot(obuf[rows(chunk * size, size), :], w, preferred_element_type=jnp.float32).astype(jnp.bfloat16)
+            for b in range(2):
+                w = wdb[1, b, pl.ds(pl.multiple_of(k * q_width, q_width), q_width), :]
+                part[:, dn_cols(k, b)] = jnp.dot(obuf[...], w, preferred_element_type=jnp.float32).astype(jnp.bfloat16)
 
     def take(sem, chunk):
         @pl.when(chunk >= 1)
@@ -269,10 +283,10 @@
                     if p == 0:
                         for i in range(len(partners)):
                             take(hfree.at[i], chunk)
-                    h[lax.rem(chunk, 2), rows(own_row(p), n2), :] = out
-                    ho[chunk, mine, :] = out
-                else:
-                    yo[mine, :] = out
+                    for i in range(2):
+                        h[lax.rem(chunk, 2), i, rows(own_row(p), n2), :] = out[:, i * half:(i + 1) * half]
+                ho[chunk, mine, :] = out
+                if stream == 1:
                     y_copy(p, chunk).start()
                 give(free.at[stream, 1, p], chunk, first_dev[col])
                 give(free.at[stream, 2, p], chunk, second_dev[col])
@@ -285,7 +299,8 @@
 
     for cp in qkv_copies():
         cp.start()
-    x_copy(0).start()
+    for cp in x_copy(0):
+        cp.start()
     for cp in wo_copies():
         cp.start()
     for chunk in range(CHUNKS):
@@ -334,7 +349,7 @@
             def _():
                 launch(dn_copies(0))
             slot = lax.rem(c * gu_tiles + j, 2)
-            both = jnp.dot(h[lax.rem(c, 2)], wgu[slot], preferred_element_type=jnp.float32)
+            both = times_h(lax.rem(c, 2), [wgu[slot, pl.ds(i * half, half)] for i in range(2)])
             gate, up = both[:, :GU], both[:, GU:]
             act[:, pl.ds(pl.multiple_of(j * GU, GU), GU)] = (gate * lax.logistic(gate) * up).astype(jnp.bfloat16)
 
@@ -351,7 +366,8 @@
             @pl.when(k + 1 < dn_tiles)
             def _():
                 launch(dn_copies(k + 1))
-            part[:, pl.ds(pl.multiple_of(k * DN, DN), DN)] = jnp.dot(act[...], wdb[lax.rem(k, 2)], preferred_element_type=jnp.float32).astype(jnp.bfloat16)
+            for b in range(2):
+                part[:, dn_cols(k, b)] = jnp.dot(act[...], wdb[lax.rem(k, 2), b], preferred_element_type=jnp.float32).astype(jnp.bfloat16)
 
             @pl.when(k + 1 == dn_tiles)
             def _():
@@ -361,6 +377,9 @@
                 def _():
                     for cp in wo_copies():
                         cp.start()
+
+    for cp in kv_copies(CHUNKS - 1):
+        cp.wait()
 
 
 def store_kernel(y_ref, k_ref, v_ref, y_out, k_out, v_out, buf, kv, get, put):
@@ -406,20 +425,20 @@
         anyspec = pl.BlockSpec(memory_space=pl.ANY)
         vmem = pl.BlockSpec(memory_space=pltpu.VMEM)
         dma, credit = pltpu.SemaphoreType.DMA, pltpu.SemaphoreType.REGULAR
-        kv = jax.ShapeDtypeStruct((total, HEAD_DIM), bf)
+        cache_shape = jax.ShapeDtypeStruct((total, HEAD_DIM), bf)
         y, keys, v = pl.pallas_call(
             functools.partial(layer_kernel, seq_len, tp_size),
-            out_shape=[jax.ShapeDtypeStruct((total, width), bf), kv, kv],
+            out_shape=[jax.ShapeDtypeStruct((total, width), bf), cache_shape, cache_shape],
             in_specs=[pl.BlockSpec(memory_space=pltpu.SMEM)] + [anyspec] * 8 + [vmem] * 6,
-            out_specs=[anyspec, vmem, vmem],
+            out_specs=[anyspec] * 3,
             scratch_shapes=[
-                pltpu.VMEM((2, width, 2 * GU), bf), pltpu.VMEM((2, inner, DN), bf), pltpu.VMEM((2, size, width), bf),
+                pltpu.VMEM((2, width, 2 * GU), bf), pltpu.VMEM((2, 2, inner, DN // 2), bf), pltpu.VMEM((2, 2, size, width // 2), bf),
                 pltpu.VMEM((size, inner), bf), pltpu.VMEM((size, width), bf),
                 pltpu.VMEM((2, size // 2, width), bf), pltpu.VMEM((2, size // 4, width), bf), pltpu.VMEM((2, size // 8, width), bf),
-                pltpu.VMEM((total, q_width), bf), pltpu.VMEM((size, q_width + HEAD_DIM), f32),
-                pltpu.VMEM((CHUNKS, size // 8, width), bf), pltpu.VMEM((size // 8, width), bf),
+                pltpu.VMEM((size, q_width), bf), pltpu.VMEM((size, q_width + HEAD_DIM), f32), pltpu.VMEM((2, size, HEAD_DIM), bf),
+                pltpu.VMEM((CHUNKS, size // 8, width), bf),
                 pltpu.VMEM((CHUNKS, 8, STAT), f32), pltpu.VMEM((CHUNKS, tp_size - 1, 8, STAT), f32), pltpu.VMEM((2, 8, STAT), f32),
-                dma((2, 2, 2)), dma((2, 2)), dma((width // DN,)), dma((3,)), dma, dma((CHUNKS, 4)), dma((4,)),
+                dma((2, 2, 2)), dma((2, 2)), dma((width // DN, 2)), dma((3,)), dma((2,)), dma((2,)), dma((CHUNKS, 4)), dma((4,)),
                 dma((CHUNKS, tp_size - 1)), dma((CHUNKS, tp_size - 1)), dma((2, CHUNKS, 6, 4)), dma((2, CHUNKS, 6, 4)),
                 credit((2, 3, 4)), credit((3,)),
             ],

time: 456 us -> 446 us (0.978)
  Pallas kernels: 455 us -> 446 us
    pallas_call x1, Pallas kernels: 439 us -> 430 us  [local_layer(): pl.pallas_call(functools.partial(layer_kernel, seq_len, tp_size), out_sha...]
where the time goes in v5:
time: 446 us
  Pallas kernels  446 us (100%)
    pallas_call x1, Pallas kernels, local_layer(): pl.pallas_call(functools.partial(layer_kernel, seq_len, tp_size), out_sha...  430 us
    pallas_call x1, Pallas kernels, store(): pl.pallas_call(store_kernel, out_shape=[jax.ShapeDtypeStruct(t.shape, t.d...  15.4 us

profile of v5, /device:TPU:0, one launch (start us, length us, event | category | flops | bytes accessed | tf_op | source)
XLA Modules:
  0.0 446.2 jit_solution(17861254369516603176)
XLA Ops:
  0.6 430.2 %shard_map.166 = (bf16[2048,5120]{1,0:T(8,128)(2,1)}, bf16[2048,128]{1,0:T(8,128)(2,1)}, bf16[2048,128]{1,0:T(8,128)(2,1)}) custom-call(s32[32]{0:T(128)} %lens_ref.1, bf16[2048,5120]{1,0:T(8,128)(2,1)} %bitcast.8, bf16[5120,640]{1,0:T(8,128)(2,1)} %wq_ref.1, bf16[5120,128]{1,0:T(8,128)(2,1)} %wk_ref.1, bf16[5120,128]{1,0:T(8,128)(2,1)} %wv_ref.1, ...), custom_call_target="tpu_custom_call" | custom-call | flops 249644974080 | bytes 424673280 | tf_op jit(solution)/shard_map/pallas_call | solution.py:429
  430.8 15.4 %shard_map.167 = (bf16[2048,5120]{1,0:T(8,128)(2,1)}, bf16[2048,128]{1,0:T(8,128)(2,1)}, bf16[2048,128]{1,0:T(8,128)(2,1)}) custom-call(bf16[2048,5120]{1,0:T(8,128)(2,1)} %get-tuple-element.9.y_ref, bf16[2048,128]{1,0:T(8,128)(2,1)} %get-tuple-element.10.k_ref, bf16[2048,128]{1,0:T(8,128)(2,1)} %get-tuple-element.11.v_ref), custom_call_target="tpu_custom_call" | custom-call | tf_op jit(solution)/shard_map/pallas_call | solution.py:406

commit v6 on v5

--- a/solution.py
+++ b/solution.py
@@ -161,7 +161,7 @@
         def _(i):
             d = pl.ds(pl.multiple_of(dst_start + i * BLK, BLK), BLK)
             s = pl.ds(pl.multiple_of(src_start + i * BLK, BLK), BLK)
-            dst[d, :] = (dst[d, :].astype(jnp.float32) + src[s, :].astype(jnp.float32)).astype(jnp.bfloat16)
+            dst[d, :] = dst[d, :] + src[s, :]
 
     def project_qkv(chunk):
         @pl.when(chunk == 0)

time: 446 us -> 444 us (level)
  no operation moved by 1% of the time
where the time goes in v6:
time: 444 us
  Pallas kernels  444 us (100%)
    pallas_call x1, Pallas kernels, local_layer(): pl.pallas_call(functools.partial(layer_kernel, seq_len, tp_size), out_sha...  428 us
    pallas_call x1, Pallas kernels, store(): pl.pallas_call(store_kernel, out_shape=[jax.ShapeDtypeStruct(t.shape, t.d...  15.4 us

profile of v6, /device:TPU:0, one launch (start us, length us, event | category | flops | bytes accessed | tf_op | source)
XLA Modules:
  0.0 444.3 jit_solution(17255257614858597063)
XLA Ops:
  0.6 428.2 %shard_map.166 = (bf16[2048,5120]{1,0:T(8,128)(2,1)}, bf16[2048,128]{1,0:T(8,128)(2,1)}, bf16[2048,128]{1,0:T(8,128)(2,1)}) custom-call(s32[32]{0:T(128)} %lens_ref.1, bf16[2048,5120]{1,0:T(8,128)(2,1)} %bitcast.8, bf16[5120,640]{1,0:T(8,128)(2,1)} %wq_ref.1, bf16[5120,128]{1,0:T(8,128)(2,1)} %wk_ref.1, bf16[5120,128]{1,0:T(8,128)(2,1)} %wv_ref.1, ...), custom_call_target="tpu_custom_call" | custom-call | flops 249644974080 | bytes 424673280 | tf_op jit(solution)/shard_map/pallas_call | solution.py:429
  428.9 15.4 %shard_map.167 = (bf16[2048,5120]{1,0:T(8,128)(2,1)}, bf16[2048,128]{1,0:T(8,128)(2,1)}, bf16[2048,128]{1,0:T(8,128)(2,1)}) custom-call(bf16[2048,5120]{1,0:T(8,128)(2,1)} %get-tuple-element.9.y_ref, bf16[2048,128]{1,0:T(8,128)(2,1)} %get-tuple-element.10.k_ref, bf16[2048,128]{1,0:T(8,128)(2,1)} %get-tuple-element.11.v_ref), custom_call_target="tpu_custom_call" | custom-call | tf_op jit(solution)/shard_map/pallas_call | solution.py:406
